TPU v7x, 512 devices: a whole 4x4x16 slice. The times are simulated.
512 devices in a mesh: seq: 128 (over x, y, z_hi, core), ch: 4 (over z_lo).
Axes of the slice: x: 4, y: 4, z: 16 (z_hi: 4, z_lo: 4; z = z_hi * 4 + z_lo), core: 2. Of those that a mesh axis runs over, the one named last changes fastest.
Arguments:
- out_gate: bfloat16 [4096, 16384], P('ch', 'seq'), may hold values from -6 to 6
- key_proj: bfloat16 [4096, 16384], P('ch', 'seq'), may hold values from -6 to 6
- value_proj: bfloat16 [4096, 16384], P('ch', 'seq'), may hold values from -6 to 6
- long_filter: bfloat16 [4096, 16384], P('ch', 'seq'), may hold values from -0.046875 to 0.046875
- skip_gain: float32 [4096], P('ch'), may hold values from -4 to 4
- residual: bfloat16 [4096, 16384], P('ch', 'seq'), may hold values from -6 to 6
- norm_gain: float32 [4096], P('ch'), may hold values from 0.5 to 1.5
Outputs:
- mixed: bfloat16 [4096, 16384], P('ch', 'seq')
- normed: bfloat16 [4096, 16384], P('ch', 'seq')
All inputs are finite; a program needn't handle non-finite values.
Results may differ from a plain program's by a relative error of at most 0.0075.
Values may be sent and summed in bfloat16 or wider, within the bound.
No kernel may reach another device: no remote copies, remote signals or barrier semaphores. Data moves between devices by JAX's collectives and lax.ppermute only.
A program may use at most 64 MiB of HBM per device.

v0:
```python
import math

import jax
import jax.numpy as jnp
import numpy as np
from jax import lax
from jax.experimental import pallas as pl
from jax.experimental.pallas import tpu as pltpu
from jax.sharding import PartitionSpec as P

D = 4096
BLOCKS = 128
WIDTH = 128
GROUP = 8
SPAN = 256

F32 = jnp.float32
BF16 = jnp.bfloat16


def split_table(table):
    high = table.astype(np.float32).astype(jnp.bfloat16)
    low = (table - high.astype(np.float64)).astype(np.float32).astype(jnp.bfloat16)
    return high, low


def angles(odd, plain):
    return ((2 * odd + 1) * plain % (2 * SPAN)).astype(np.float64) * (math.pi / SPAN)


def tables(arrival, departure):
    steps = np.arange(WIDTH)
    freqs = np.arange(WIDTH)
    phase = angles(freqs[None, :], steps[:, None])
    enter = np.concatenate([np.cos(phase), -np.sin(phase)], axis=1)
    enter_hi, enter_lo = split_table(enter)
    enter_both = np.concatenate([enter_hi, enter_lo], axis=0)

    phase = angles(freqs[:, None], arrival[None, :])
    over = np.concatenate([np.cos(phase), np.sin(phase)], axis=0)
    over_hi, over_lo = split_table(over)
    over_hi = np.concatenate([over_hi, over_hi], axis=1)
    over_lo = np.concatenate([over_lo, over_lo], axis=1)

    def back_rows(blocks):
        phase = angles(freqs[None, :], blocks[:, None])
        rows = np.concatenate([np.cos(phase), np.sin(phase)], axis=1) / SPAN
        return np.where(blocks[:, None] >= 0, rows, 0.0)

    back = np.concatenate([back_rows(departure), back_rows(departure - 1)], axis=0)
    back_hi, back_lo = split_table(back)

    def leave_rows(places):
        phase = angles(freqs[:, None], places[None, :])
        return np.concatenate([np.cos(phase), -np.sin(phase)], axis=0) * (2.0 / SPAN)

    leave = np.concatenate([leave_rows(steps), leave_rows(steps + WIDTH)], axis=0)
    leave_hi, leave_lo = split_table(leave)
    return enter_both, over_hi, over_lo, back_hi, back_lo, leave_hi, leave_lo


def dot(left, right):
    return jnp.dot(left, right, preferred_element_type=F32)


def halves(value):
    high = value.astype(BF16)
    return high, (value - high.astype(F32)).astype(BF16)


def convolve_kernel(
    rows_ref, enter_ref, over_hi_ref, over_lo_ref, back_hi_ref, back_lo_ref,
    leave_hi_ref, leave_lo_ref, out_ref, real_ref, imag_ref, time_ref,
):
    chunk = 256
    for start in range(0, 2 * GROUP * BLOCKS, chunk):
        piece = rows_ref[start : start + chunk, :]
        spectrum = dot(jnp.concatenate([piece, piece], axis=1), enter_ref[...])
        real_ref[start : start + chunk, :] = spectrum[:, :WIDTH]
        imag_ref[start : start + chunk, :] = spectrum[:, WIDTH:]

    def over_blocks(row):
        rows = pl.ds(row, BLOCKS, stride=2 * GROUP)
        high, low = halves(jnp.concatenate([real_ref[rows, :], imag_ref[rows, :]], axis=1))
        both = jnp.concatenate([high, low], axis=0)
        sums = dot(over_hi_ref[...], both) + dot(over_lo_ref[...], both)
        cos_re, cos_im = sums[:WIDTH, :WIDTH], sums[:WIDTH, WIDTH:]
        sin_re, sin_im = sums[WIDTH:, :WIDTH], sums[WIDTH:, WIDTH:]
        return cos_re + sin_im, cos_im - sin_re, cos_re - sin_im, cos_im + sin_re

    for chan in range(GROUP):
        xp_re, xp_im, xm_re, xm_im = over_blocks(chan)
        hp_re, hp_im, hm_re, hm_im = over_blocks(GROUP + chan)
        pp_re = xp_re * hp_re - xp_im * hp_im
        pp_im = xp_re * hp_im + xp_im * hp_re
        pm_re = xm_re * hm_re - xm_im * hm_im
        pm_im = xm_re * hm_im + xm_im * hm_re
        joint = jnp.concatenate(
            [
                jnp.concatenate([pp_re + pm_re, pp_im + pm_im], axis=1),
                jnp.concatenate([pm_im - pp_im, pp_re - pm_re], axis=1),
            ],
            axis=0,
        )
        joint_hi, joint_lo = halves(joint)
        blocks = (
            dot(back_hi_ref[...], joint_hi)
            + dot(back_hi_ref[...], joint_lo)
            + dot(back_lo_ref[...], joint_hi)
        )
        pair_hi, pair_lo = halves(
            jnp.concatenate([blocks[:BLOCKS, :], blocks[BLOCKS:, :]], axis=1)
        )
        time_ref[pl.ds(chan, BLOCKS, stride=GROUP), :] = (
            dot(pair_hi, leave_hi_ref[...])
            + dot(pair_lo, leave_hi_ref[...])
            + dot(pair_hi, leave_lo_ref[...])
        )
    out_ref[...] = time_ref[...].astype(BF16)


def convolve(rows, consts, interpret=False):
    return pl.pallas_call(
        convolve_kernel,
        out_shape=jax.ShapeDtypeStruct((GROUP * BLOCKS, WIDTH), BF16),
        scratch_shapes=[
            pltpu.VMEM((2 * GROUP * BLOCKS, WIDTH), F32),
            pltpu.VMEM((2 * GROUP * BLOCKS, WIDTH), F32),
            pltpu.VMEM((GROUP * BLOCKS, WIDTH), F32),
        ],
        name="convolve",
        interpret=interpret,
    )(rows, *consts)


def on_device(out_gate, key_proj, value_proj, long_filter, skip_gain, residual, norm_gain):
    chans, width = key_proj.shape
    blocks = lax.axis_size("seq")
    order = np.arange(blocks)
    consts = [jnp.asarray(table) for table in tables(order, order)]
    gated = lax.reduce_precision(key_proj.astype(F32) * value_proj.astype(F32), 8, 7)
    both = jnp.concatenate(
        [gated.astype(BF16).reshape(blocks, GROUP, width), long_filter.reshape(blocks, GROUP, width)],
        axis=1,
    )
    arrived = lax.all_to_all(both, "seq", 0, 0, tiled=True)
    convolved = convolve(arrived.reshape(2 * GROUP * blocks, width), consts)
    convolved = lax.all_to_all(convolved.reshape(blocks, GROUP, width), "seq", 0, 0, tiled=True)
    convolved = convolved.reshape(chans, width).astype(F32)
    total = residual.astype(F32) + out_gate.astype(F32) * (convolved + skip_gain[:, None] * gated)
    squares = jnp.sum(total * total, axis=0, keepdims=True)
    count = lax.axis_size("ch")
    squares = jnp.sum(
        lax.all_to_all(
            jnp.broadcast_to(squares[None], (count, 1, width)), "ch", 0, 0, tiled=True
        ),
        axis=0,
    )
    normed = total * lax.rsqrt(squares / D + 1e-06) * norm_gain[:, None]
    return (total.astype(BF16), normed.astype(BF16))


def solution(mesh):
    return jax.shard_map(
        on_device,
        mesh=mesh,
        in_specs=(
            P("ch", "seq"),
            P("ch", "seq"),
            P("ch", "seq"),
            P("ch", "seq"),
            P("ch"),
            P("ch", "seq"),
            P("ch"),
        ),
        out_specs=(P("ch", "seq"), P("ch", "seq")),
        check_vma=False,
    )
```

profile of v0, /device:TPU:1, one launch (start us, length us, event | category | flops | bytes accessed | tf_op | source)
XLA Modules:
  0.0 110.8 jit_solution(9965521536504814802)
XLA Ops:
  0.6 0.0 copy-start.2
  0.6 1.1 %fusion.3 = bf16[128,8,128]{2,1,0:T(8,128)(2,1)S(1)} fusion(bf16[1024,128]{1,0:T(8,128)(2,1)} %param.16, bf16[1024,128]{1,0:T(8,128)(2,1)} %param.15), kind=kLoop, calls=%fused_computation.8 | loop fusion | flops 655360 | bytes 786432 | tf_op jit(solution)/shard_map/reshape | solution.py:143
  1.8 0.0 copy-done.2
  1.8 0.1 pad_maximum_fusion
  1.9 54.0 %all_to_all.15 = bf16[128,16,128]{2,1,0:T(8,128)(2,1)} all-to-all(bf16[128,16,128]{2,1,0:T(8,128)(2,1)S(1)} %pad_maximum_fusion), channel_id=1, replica_groups=mesh['seq'=128,'ch'=4] {'seq'}, dimensions={0} | all-to-all | bytes 1048576 | tf_op jit(solution)/shard_map/all_to_all | solution.py:146
  55.9 0.0 copy-start.3
  55.9 0.0 copy-start.4
  55.9 0.0 copy-start.5
  55.9 9.1 %convolve.1 = bf16[1024,128]{1,0:T(8,128)(2,1)} custom-call(bf16[2048,128]{1,0:T(8,128)(2,1)} %bitcast.10, bf16[256,256]{1,0:T(8,128)(2,1)} %constant.21.clone.enter_ref, bf16[256,256]{1,0:T(8,128)(2,1)} %constant.22.clone.over_hi_ref, bf16[256,256]{1,0:T(8,128)(2,1)} %constant.23.clone.over_lo_ref, bf16[256,256]{1,0:T(8,128)(2,1)} %constant.24.clone.back_hi_ref, ...), custom_call_target="tpu_custom_call" | custom-call | tf_op jit(solution)/shard_map/convolve/pallas_call | solution.py:123
  65.0 0.0 copy-start
  65.0 0.0 copy-start.1
  65.0 32.0 %all_to_all.16 = bf16[128,8,128]{2,1,0:T(8,128)(2,1)S(1)} all-to-all(bf16[128,8,128]{2,1,0:T(8,128)(2,1)} %bitcast.11), channel_id=1, replica_groups=mesh['seq'=128,'ch'=4] {'seq'}, dimensions={0} | all-to-all | bytes 524288 | tf_op jit(solution)/shard_map/all_to_all | solution.py:148
  97.0 0.0 copy-done.3
  97.0 0.0 copy-done.4
  97.0 0.0 copy-done.5
  97.0 0.0 copy-done
  97.0 0.0 copy-done.1
  97.0 0.3 multiply_reduce_fusion
  97.4 11.8 %all_to_all.17 = f32[4,1,128]{2,1,0:T(1,128)S(1)} all-to-all(f32[4,1,128]{2,1,0:T(1,128)S(1)} %broadcast_in_dim.2), channel_id=1, replica_groups=mesh['seq'=128,'ch'=4] {'ch'}, dimensions={0} | all-to-all | bytes 4096 | tf_op jit(solution)/shard_map/all_to_all | solution.py:154
  109.2 0.0 copy-start.6
  109.2 0.7 copy-done.6
  109.9 1.0 multiply_convert_fusion
  (3 shorter events, 0.0 us)
Async XLA Ops:
  0.6 1.2 %copy-start.2 = (bf16[1024,128]{1,0:T(8,128)(2,1)S(1)}, bf16[1024,128]{1,0:T(8,128)(2,1)}, u32[]{:S(2)}) copy-start(bf16[1024,128]{1,0:T(8,128)(2,1)} %param.17) | copy-start | bytes 786436
  55.9 41.1 %copy-start.3 = (bf16[1024,128]{1,0:T(8,128)(2,1)S(1)}, bf16[1024,128]{1,0:T(8,128)(2,1)}, u32[]{:S(2)}) copy-start(bf16[1024,128]{1,0:T(8,128)(2,1)} %param.14) | copy-start | bytes 786436
  55.9 41.1 %copy-start.4 = (bf16[1024,128]{1,0:T(8,128)(2,1)S(1)}, bf16[1024,128]{1,0:T(8,128)(2,1)}, u32[]{:S(2)}) copy-start(bf16[1024,128]{1,0:T(8,128)(2,1)} %param.19) | copy-start | bytes 786436
  55.9 41.1 %copy-start.5 = (f32[1024]{0:T(1024)S(1)}, f32[1024]{0:T(1024)}, u32[]{:S(2)}) copy-start(f32[1024]{0:T(1024)} %param.18) | copy-start | bytes 12292
  65.0 32.0 %copy-start = (bf16[1024,128]{1,0:T(8,128)(2,1)S(1)}, bf16[1024,128]{1,0:T(8,128)(2,1)}, u32[]{:S(2)}) copy-start(bf16[1024,128]{1,0:T(8,128)(2,1)} %param.16) | copy-start | bytes 786436
  65.0 32.0 %copy-start.1 = (bf16[1024,128]{1,0:T(8,128)(2,1)S(1)}, bf16[1024,128]{1,0:T(8,128)(2,1)}, u32[]{:S(2)}) copy-start(bf16[1024,128]{1,0:T(8,128)(2,1)} %param.15) | copy-start | bytes 786436
  109.2 0.7 copy-start.6
where the time goes:
time: 111 us
  blocking collectives  97.8 us (88%)
  Pallas kernels  9.1 us (8%)
  other arithmetic  2.55 us (2%)
    all_to_all x1, blocking collectives, on_device(): arrived = lax.all_to_all(both, 'seq', 0, 0, tiled=True)  54 us
    all_to_all x1, blocking collectives, on_device(): lax.all_to_all(convolved.reshape(blocks, GROUP, width), 'seq', 0, 0, tile...  32 us
    all_to_all x1, blocking collectives, on_device(): lax.all_to_all(jnp.broadcast_to(squares[None], (count, 1, width)), 'ch',...  11.8 us
    pallas_call x1, Pallas kernels, convolve(): pl.pallas_call(convolve_kernel, out_shape=jax.ShapeDtypeStruct((GROUP * B...  9.1 us

commit v1 on v0

v1 whole, which is shorter than its diff:
```python
import math

import jax
import jax.numpy as jnp
import numpy as np
from jax import lax
from jax.experimental import pallas as pl
from jax.experimental.pallas import tpu as pltpu
from jax.sharding import PartitionSpec as P

D = 4096
BLOCKS = 128
WIDTH = 128
GROUP = 8
SPAN = 256

F32 = jnp.float32
BF16 = jnp.bfloat16


def split_table(table):
    high = table.astype(np.float32).astype(jnp.bfloat16)
    low = (table - high.astype(np.float64)).astype(np.float32).astype(jnp.bfloat16)
    return high, low


def angles(odd, plain):
    return ((2 * odd + 1) * plain % (2 * SPAN)).astype(np.float64) * (math.pi / SPAN)


def tables():
    steps = np.arange(WIDTH)
    phase = angles(steps[None, :], steps[:, None])
    enter = np.concatenate([np.cos(phase), -np.sin(phase)], axis=1)
    enter = np.concatenate(split_table(enter), axis=0)

    phase = angles(steps[:, None], steps[None, :])
    over = np.concatenate([np.cos(phase), np.sin(phase)], axis=0)
    over_hi, over_lo = (np.concatenate([part, part], axis=1) for part in split_table(over))

    phase = angles(steps[None, :], steps[:, None])
    back = np.concatenate([np.cos(phase), np.sin(phase)], axis=1) / SPAN
    back = np.concatenate(split_table(back), axis=0)

    phase = angles(steps[:, None], np.arange(SPAN)[None, :])
    leave = np.concatenate([np.cos(phase), -np.sin(phase)], axis=0) * (2.0 / SPAN)
    leave_hi, leave_lo = split_table(leave)
    return enter, over_hi, over_lo, back, leave_hi, leave_lo


def dot(left, right):
    return jnp.dot(left, right, preferred_element_type=F32)


def halves(value):
    high = value.astype(BF16)
    return high, (value - high.astype(F32)).astype(BF16)


def convolve_kernel(
    rows_ref, enter_ref, over_hi_ref, over_lo_ref, back_ref, leave_hi_ref, leave_lo_ref,
    out_ref, real_ref, imag_ref, joint_hi_ref, joint_lo_ref, pair_hi_ref, pair_lo_ref,
    early_ref, late_ref,
):
    chunk = 256
    for start in range(0, 2 * GROUP * BLOCKS, chunk):
        piece = rows_ref[start : start + chunk, :]
        spectrum = dot(jnp.concatenate([piece, piece], axis=1), enter_ref[...])
        real_ref[start : start + chunk, :] = spectrum[:, :WIDTH]
        imag_ref[start : start + chunk, :] = spectrum[:, WIDTH:]

    def over_blocks(row):
        rows = pl.ds(row, BLOCKS, stride=2 * GROUP)
        high, low = halves(jnp.concatenate([real_ref[rows, :], imag_ref[rows, :]], axis=1))
        both = jnp.concatenate([high, low], axis=0)
        sums = dot(over_hi_ref[...], both) + dot(over_lo_ref[...], both)
        cos_re, cos_im = sums[:WIDTH, :WIDTH], sums[:WIDTH, WIDTH:]
        sin_re, sin_im = sums[WIDTH:, :WIDTH], sums[WIDTH:, WIDTH:]
        return cos_re + sin_im, cos_im - sin_re, cos_re - sin_im, cos_im + sin_re

    for chan in range(GROUP):
        xp_re, xp_im, xm_re, xm_im = over_blocks(chan)
        hp_re, hp_im, hm_re, hm_im = over_blocks(GROUP + chan)
        pp_re = xp_re * hp_re - xp_im * hp_im
        pp_im = xp_re * hp_im + xp_im * hp_re
        pm_re = xm_re * hm_re - xm_im * hm_im
        pm_im = xm_re * hm_im + xm_im * hm_re
        quarters = (pp_re + pm_re, pp_im + pm_im, pm_im - pp_im, pp_re - pm_re)
        for place, quarter in enumerate(quarters):
            rows = pl.ds((2 * chan + place // 2) * WIDTH, WIDTH)
            lanes = pl.ds(place % 2 * WIDTH, WIDTH)
            joint_hi_ref[rows, lanes], joint_lo_ref[rows, lanes] = halves(quarter)

    for chan in range(GROUP):
        joint = pl.ds(chan * SPAN, SPAN)
        rows = pl.ds(chan * BLOCKS, BLOCKS)
        sums = dot(back_ref[...], joint_hi_ref[joint, :])
        low = dot(back_ref[:BLOCKS, :], joint_lo_ref[joint, :])
        pair_hi_ref[rows, :], pair_lo_ref[rows, :] = halves(sums[:BLOCKS] + sums[BLOCKS:] + low)

    late_ref[pl.ds(0, GROUP), :] = jnp.zeros((GROUP, WIDTH), F32)
    for chan in range(GROUP):
        rows = pl.ds(chan * BLOCKS, BLOCKS)
        high, low = pair_hi_ref[rows, :], pair_lo_ref[rows, :]
        timeline = (
            dot(high, leave_hi_ref[...])
            + dot(low, leave_hi_ref[...])
            + dot(high, leave_lo_ref[...])
        )
        early_ref[pl.ds(chan, BLOCKS, stride=GROUP), :] = timeline[:, :WIDTH]
        late_ref[pl.ds(GROUP + chan, BLOCKS, stride=GROUP), :] = timeline[:, WIDTH:]
    out_ref[...] = (early_ref[...] + late_ref[: GROUP * BLOCKS, :]).astype(BF16)


def in_vmem(value):
    return pltpu.with_memory_space_constraint(value, pltpu.VMEM)


def convolve(rows, consts):
    return pl.pallas_call(
        convolve_kernel,
        out_shape=pltpu.VMEM((GROUP * BLOCKS, WIDTH), BF16),
        scratch_shapes=[
            pltpu.VMEM((2 * GROUP * BLOCKS, WIDTH), F32),
            pltpu.VMEM((2 * GROUP * BLOCKS, WIDTH), F32),
            pltpu.VMEM((GROUP * SPAN, SPAN), BF16),
            pltpu.VMEM((GROUP * SPAN, SPAN), BF16),
            pltpu.VMEM((GROUP * BLOCKS, SPAN), BF16),
            pltpu.VMEM((GROUP * BLOCKS, SPAN), BF16),
            pltpu.VMEM((GROUP * BLOCKS, WIDTH), F32),
            pltpu.VMEM((GROUP * (BLOCKS + 1), WIDTH), F32),
        ],
        name="convolve",
    )(in_vmem(rows), *[in_vmem(table) for table in consts])


def on_device(out_gate, key_proj, value_proj, long_filter, skip_gain, residual, norm_gain):
    chans, width = key_proj.shape
    blocks = lax.axis_size("seq")
    consts = [jnp.asarray(table) for table in tables()]
    gated = lax.reduce_precision(key_proj.astype(F32) * value_proj.astype(F32), 8, 7)
    both = jnp.concatenate(
        [gated.astype(BF16).reshape(blocks, GROUP, width), long_filter.reshape(blocks, GROUP, width)],
        axis=1,
    )
    arrived = lax.all_to_all(both, "seq", 0, 0, tiled=True)
    convolved = convolve(arrived.reshape(2 * GROUP * blocks, width), consts)
    convolved = lax.all_to_all(convolved.reshape(blocks, GROUP, width), "seq", 0, 0, tiled=True)
    convolved = convolved.reshape(chans, width).astype(F32)
    total = residual.astype(F32) + out_gate.astype(F32) * (convolved + skip_gain[:, None] * gated)
    mixed, scaled, squares = lax.optimization_barrier(
        (
            total.astype(BF16),
            total * norm_gain[:, None],
            jnp.sum(total * total, axis=0, keepdims=True),
        )
    )
    count = lax.axis_size("ch")
    squares = jnp.sum(
        lax.all_to_all(
            jnp.broadcast_to(squares[None], (count, 1, width)), "ch", 0, 0, tiled=True
        ),
        axis=0,
    )
    normed = scaled * lax.rsqrt(squares / D + 1e-06)
    return (mixed, normed.astype(BF16))


def solution(mesh):
    return jax.shard_map(
        on_device,
        mesh=mesh,
        in_specs=(
            P("ch", "seq"),
            P("ch", "seq"),
            P("ch", "seq"),
            P("ch", "seq"),
            P("ch"),
            P("ch", "seq"),
            P("ch"),
        ),
        out_specs=(P("ch", "seq"), P("ch", "seq")),
        check_vma=False,
    )
```

time: 111 us -> 106 us (0.955)
  Pallas kernels: 9.1 us -> 3.08 us
    pallas_call x1, Pallas kernels: 9.1 us -> 3.08 us  [convolve(): pl.pallas_call(convolve_kernel, out_shape=pltpu.VMEM((GROUP * BLOCKS, WID...]
where the time goes in v1:
time: 106 us; the launch traced here: 105 us
  blocking collectives  97.8 us (92%)
  other arithmetic  3.19 us (3%)
  Pallas kernels  3.08 us (3%)
    all_to_all x1, blocking collectives, on_device(): arrived = lax.all_to_all(both, 'seq', 0, 0, tiled=True)  54.1 us
    all_to_all x1, blocking collectives, on_device(): lax.all_to_all(convolved.reshape(blocks, GROUP, width), 'seq', 0, 0, tile...  32.1 us
    all_to_all x1, blocking collectives, on_device(): lax.all_to_all(jnp.broadcast_to(squares[None], (count, 1, width)), 'ch',...  11.6 us
    pallas_call x1, Pallas kernels, convolve(): pl.pallas_call(convolve_kernel, out_shape=pltpu.VMEM((GROUP * BLOCKS, WID...  3.08 us

profile of v1, /device:TPU:1, one launch (start us, length us, event | category | flops | bytes accessed | tf_op | source)
XLA Modules:
  0.0 105.3 jit_solution(17522890104504947196)
XLA Ops:
  0.6 0.0 copy-start.8
  0.6 1.1 %fusion.3 = bf16[128,8,128]{2,1,0:T(8,128)(2,1)S(1)} fusion(bf16[1024,128]{1,0:T(8,128)(2,1)} %param.15, bf16[1024,128]{1,0:T(8,128)(2,1)} %param.14), kind=kLoop, calls=%fused_computation.8 | loop fusion | flops 655360 | bytes 786432 | tf_op jit(solution)/shard_map/reshape | solution.py:143
  1.8 0.0 copy-done.8
  1.8 0.1 pad_maximum_fusion
  1.9 0.0 copy-start
  1.9 0.0 copy-start.1
  1.9 0.0 copy-start.2
  1.9 0.0 copy-start.3
  1.9 0.0 copy-start.4
  2.0 0.0 copy-start.5
  2.0 54.1 %all_to_all.15 = bf16[128,16,128]{2,1,0:T(8,128)(2,1)S(1)} all-to-all(bf16[128,16,128]{2,1,0:T(8,128)(2,1)S(1)} %pad_maximum_fusion), channel_id=1, replica_groups=mesh['seq'=128,'ch'=4] {'seq'}, dimensions={0} | all-to-all | bytes 1048576 | tf_op jit(solution)/shard_map/all_to_all | solution.py:146
  56.0 0.0 copy-done
  56.0 0.0 copy-done.1
  56.0 0.0 copy-done.2
  56.0 0.0 copy-done.3
  56.0 0.0 copy-done.4
  56.1 0.0 copy-done.5
  56.1 0.0 copy-start.9
  56.1 0.0 copy-start.10
  56.1 0.0 copy-start.11
  56.1 3.1 %convolve.1 = bf16[1024,128]{1,0:T(8,128)(2,1)S(1)} custom-call(bf16[2048,128]{1,0:T(8,128)(2,1)S(1)} %bitcast.12, bf16[256,256]{1,0:T(8,128)(2,1)S(1)} %copy-done.5, bf16[256,256]{1,0:T(8,128)(2,1)S(1)} %copy-done.4, bf16[256,256]{1,0:T(8,128)(2,1)S(1)} %copy-done.3, bf16[256,256]{1,0:T(8,128)(2,1)S(1)} %copy-done.2, bf16[256,256]{1,0:T(8,128)(2,1)S(1)} %copy-done.1, ...), custom_call_target="tpu_custom_call" | custom-call | tf_op jit(solution)/shard_map/convolve/pallas_call | solution.py:120
  59.2 0.0 copy-start.6
  59.2 0.0 copy-start.7
  59.2 32.1 %all_to_all.16 = bf16[128,8,128]{2,1,0:T(8,128)(2,1)S(1)} all-to-all(bf16[128,8,128]{2,1,0:T(8,128)(2,1)S(1)} %bitcast.13), channel_id=1, replica_groups=mesh['seq'=128,'ch'=4] {'seq'}, dimensions={0} | all-to-all | bytes 524288 | tf_op jit(solution)/shard_map/all_to_all | solution.py:148
  91.3 0.0 copy-done.9
  91.3 0.0 copy-done.10
  91.3 0.0 copy-done.11
  91.3 0.0 copy-done.6
  91.3 0.0 copy-done.7
  91.4 0.0 copy-start.12
  91.4 0.3 multiply_reduce_fusion
  91.7 0.4 copy-done.12
  92.0 0.9 broadcast_multiply_fusion
  92.9 11.6 %all_to_all.17 = f32[4,1,128]{2,1,0:T(1,128)S(1)} all-to-all(f32[4,1,128]{2,1,0:T(1,128)S(1)} %broadcast_in_dim.15), channel_id=1, replica_groups=mesh['seq'=128,'ch'=4] {'ch'}, dimensions={0} | all-to-all | bytes 4096 | tf_op jit(solution)/shard_map/all_to_all | solution.py:160
  104.6 0.7 multiply_convert_fusion
  (3 shorter events, 0.0 us)
Async XLA Ops:
  0.6 1.2 %copy-start.8 = (bf16[1024,128]{1,0:T(8,128)(2,1)S(1)}, bf16[1024,128]{1,0:T(8,128)(2,1)}, u32[]{:S(2)}) copy-start(bf16[1024,128]{1,0:T(8,128)(2,1)} %param.16) | copy-start | bytes 786436
  1.9 54.1 %copy-start = (bf16[256,256]{1,0:T(8,128)(2,1)S(1)}, bf16[256,256]{1,0:T(8,128)(2,1)}, u32[]{:S(2)}) copy-start(bf16[256,256]{1,0:T(8,128)(2,1)} %constant.24.clone.leave_lo_ref) | copy-start | bytes 393220
  1.9 54.1 %copy-start.1 = (bf16[256,256]{1,0:T(8,128)(2,1)S(1)}, bf16[256,256]{1,0:T(8,128)(2,1)}, u32[]{:S(2)}) copy-start(bf16[256,256]{1,0:T(8,128)(2,1)} %constant.23.clone.leave_hi_ref) | copy-start | bytes 393220
  1.9 54.1 %copy-start.2 = (bf16[256,256]{1,0:T(8,128)(2,1)S(1)}, bf16[256,256]{1,0:T(8,128)(2,1)}, u32[]{:S(2)}) copy-start(bf16[256,256]{1,0:T(8,128)(2,1)} %constant.22.clone.back_ref) | copy-start | bytes 393220
  1.9 54.1 %copy-start.3 = (bf16[256,256]{1,0:T(8,128)(2,1)S(1)}, bf16[256,256]{1,0:T(8,128)(2,1)}, u32[]{:S(2)}) copy-start(bf16[256,256]{1,0:T(8,128)(2,1)} %constant.21.clone.over_lo_ref) | copy-start | bytes 393220
  1.9 54.1 %copy-start.4 = (bf16[256,256]{1,0:T(8,128)(2,1)S(1)}, bf16[256,256]{1,0:T(8,128)(2,1)}, u32[]{:S(2)}) copy-start(bf16[256,256]{1,0:T(8,128)(2,1)} %constant.20.clone.over_hi_ref) | copy-start | bytes 393220
  2.0 54.1 %copy-start.5 = (bf16[256,256]{1,0:T(8,128)(2,1)S(1)}, bf16[256,256]{1,0:T(8,128)(2,1)}, u32[]{:S(2)}) copy-start(bf16[256,256]{1,0:T(8,128)(2,1)} %constant.19.clone.enter_ref) | copy-start | bytes 393220
  56.1 35.3 %copy-start.9 = (bf16[1024,128]{1,0:T(8,128)(2,1)S(1)}, bf16[1024,128]{1,0:T(8,128)(2,1)}, u32[]{:S(2)}) copy-start(bf16[1024,128]{1,0:T(8,128)(2,1)} %param.13) | copy-start | bytes 786436
  56.1 35.3 %copy-start.10 = (bf16[1024,128]{1,0:T(8,128)(2,1)S(1)}, bf16[1024,128]{1,0:T(8,128)(2,1)}, u32[]{:S(2)}) copy-start(bf16[1024,128]{1,0:T(8,128)(2,1)} %param.18) | copy-start | bytes 786436
  56.1 35.2 %copy-start.11 = (f32[1024]{0:T(1024)S(1)}, f32[1024]{0:T(1024)}, u32[]{:S(2)}) copy-start(f32[1024]{0:T(1024)} %param.17) | copy-start | bytes 12292
  59.2 32.2 %copy-start.6 = (bf16[1024,128]{1,0:T(8,128)(2,1)S(1)}, bf16[1024,128]{1,0:T(8,128)(2,1)}, u32[]{:S(2)}) copy-start(bf16[1024,128]{1,0:T(8,128)(2,1)} %param.15) | copy-start | bytes 786436
  59.2 32.1 %copy-start.7 = (bf16[1024,128]{1,0:T(8,128)(2,1)S(1)}, bf16[1024,128]{1,0:T(8,128)(2,1)}, u32[]{:S(2)}) copy-start(bf16[1024,128]{1,0:T(8,128)(2,1)} %param.14) | copy-start | bytes 786436
  91.4 0.7 copy-start.12

commit v2 on v1

--- a/solution.py
+++ b/solution.py
@@ -58,8 +58,8 @@
 
 
 def convolve_kernel(
-    rows_ref, enter_ref, over_hi_ref, over_lo_ref, back_ref, leave_hi_ref, leave_lo_ref,
-    out_ref, real_ref, imag_ref, joint_hi_ref, joint_lo_ref, pair_hi_ref, pair_lo_ref,
+    rows_ref, gain_ref, enter_ref, over_hi_ref, over_lo_ref, back_ref, leave_hi_ref,
+    leave_lo_ref, out_ref, kept_ref, real_ref, imag_ref, joint_hi_ref, joint_lo_ref, pair_hi_ref, pair_lo_ref,
     early_ref, late_ref,
 ):
     chunk = 256
@@ -109,6 +109,7 @@
         )
         early_ref[pl.ds(chan, BLOCKS, stride=GROUP), :] = timeline[:, :WIDTH]
         late_ref[pl.ds(GROUP + chan, BLOCKS, stride=GROUP), :] = timeline[:, WIDTH:]
+    kept_ref[...] = gain_ref[...]
     out_ref[...] = (early_ref[...] + late_ref[: GROUP * BLOCKS, :]).astype(BF16)
 
 
@@ -116,10 +117,13 @@
     return pltpu.with_memory_space_constraint(value, pltpu.VMEM)
 
 
-def convolve(rows, consts):
+def convolve(rows, gain, consts):
     return pl.pallas_call(
         convolve_kernel,
-        out_shape=pltpu.VMEM((GROUP * BLOCKS, WIDTH), BF16),
+        out_shape=(
+            pltpu.VMEM((GROUP * BLOCKS, WIDTH), BF16),
+            pltpu.VMEM(gain.shape, F32),
+        ),
         scratch_shapes=[
             pltpu.VMEM((2 * GROUP * BLOCKS, WIDTH), F32),
             pltpu.VMEM((2 * GROUP * BLOCKS, WIDTH), F32),
@@ -131,7 +135,7 @@
             pltpu.VMEM((GROUP * (BLOCKS + 1), WIDTH), F32),
         ],
         name="convolve",
-    )(in_vmem(rows), *[in_vmem(table) for table in consts])
+    )(in_vmem(rows), in_vmem(gain), *[in_vmem(table) for table in consts])
 
 
 def on_device(out_gate, key_proj, value_proj, long_filter, skip_gain, residual, norm_gain):
@@ -144,17 +148,15 @@
         axis=1,
     )
     arrived = lax.all_to_all(both, "seq", 0, 0, tiled=True)
-    convolved = convolve(arrived.reshape(2 * GROUP * blocks, width), consts)
+    convolved, gain = convolve(
+        arrived.reshape(2 * GROUP * blocks, width),
+        norm_gain.reshape(chans // WIDTH, WIDTH),
+        consts,
+    )
     convolved = lax.all_to_all(convolved.reshape(blocks, GROUP, width), "seq", 0, 0, tiled=True)
     convolved = convolved.reshape(chans, width).astype(F32)
     total = residual.astype(F32) + out_gate.astype(F32) * (convolved + skip_gain[:, None] * gated)
-    mixed, scaled, squares = lax.optimization_barrier(
-        (
-            total.astype(BF16),
-            total * norm_gain[:, None],
-            jnp.sum(total * total, axis=0, keepdims=True),
-        )
-    )
+    squares = jnp.sum(total * total, axis=0, keepdims=True)
     count = lax.axis_size("ch")
     squares = jnp.sum(
         lax.all_to_all(
@@ -162,8 +164,8 @@
         ),
         axis=0,
     )
-    normed = scaled * lax.rsqrt(squares / D + 1e-06)
-    return (mixed, normed.astype(BF16))
+    normed = total * lax.rsqrt(squares / D + 1e-06) * gain.reshape(chans)[:, None]
+    return (total.astype(BF16), normed.astype(BF16))
 
 
 def solution(mesh):

time: 106 us -> 105 us (level)
  no operation moved by 1% of the time
where the time goes in v2:
time: 105 us; the launch traced here: 104 us
  blocking collectives  97.7 us (93%)
  Pallas kernels  3.14 us (3%)
  other arithmetic  2.56 us (2%)
    all_to_all x1, blocking collectives, on_device(): arrived = lax.all_to_all(both, 'seq', 0, 0, tiled=True)  54.1 us
    all_to_all x1, blocking collectives, on_device(): lax.all_to_all(convolved.reshape(blocks, GROUP, width), 'seq', 0, 0, tile...  32.4 us
    all_to_all x1, blocking collectives, on_device(): lax.all_to_all(jnp.broadcast_to(squares[None], (count, 1, width)), 'ch',...  11.3 us
    pallas_call x1, Pallas kernels, convolve(): pl.pallas_call(convolve_kernel, out_shape=(pltpu.VMEM((GROUP * BLOCKS, WI...  3.14 us

profile of v2, /device:TPU:1, one launch (start us, length us, event | category | flops | bytes accessed | tf_op | source)
XLA Modules:
  0.0 104.4 jit_solution(3138817589853408729)
XLA Ops:
  0.6 0.0 copy-start.9
  0.6 1.1 %fusion.3 = bf16[128,8,128]{2,1,0:T(8,128)(2,1)S(1)} fusion(bf16[1024,128]{1,0:T(8,128)(2,1)} %param.15, bf16[1024,128]{1,0:T(8,128)(2,1)} %param.14), kind=kLoop, calls=%fused_computation.8 | loop fusion | flops 655360 | bytes 786432 | tf_op jit(solution)/shard_map/reshape | solution.py:147
  1.8 0.0 copy-done.9
  1.8 0.1 pad_maximum_fusion
  1.9 0.0 copy-start
  1.9 0.0 copy-start.1
  1.9 0.0 copy-start.2
  1.9 0.0 copy-start.3
  1.9 0.0 copy-start.4
  2.0 0.0 copy-start.5
  2.0 0.0 copy-start.6
  2.0 54.1 %all_to_all.15 = bf16[128,16,128]{2,1,0:T(8,128)(2,1)S(1)} all-to-all(bf16[128,16,128]{2,1,0:T(8,128)(2,1)S(1)} %pad_maximum_fusion), channel_id=1, replica_groups=mesh['seq'=128,'ch'=4] {'seq'}, dimensions={0} | all-to-all | bytes 1048576 | tf_op jit(solution)/shard_map/all_to_all | solution.py:150
  56.0 0.0 copy-done
  56.0 0.0 copy-done.1
  56.0 0.0 copy-done.2
  56.0 0.0 copy-done.3
  56.1 0.0 copy-done.4
  56.1 0.0 copy-done.5
  56.1 0.0 copy-done.6
  56.1 0.0 copy-start.10
  56.1 0.0 copy-start.11
  56.1 0.0 copy-start.12
  56.1 3.1 %convolve.1 = (bf16[1024,128]{1,0:T(8,128)(2,1)S(1)}, f32[8,128]{1,0:T(8,128)S(1)}) custom-call(bf16[2048,128]{1,0:T(8,128)(2,1)S(1)} %bitcast.12, f32[8,128]{1,0:T(8,128)S(1)} %bitcast.14, bf16[256,256]{1,0:T(8,128)(2,1)S(1)} %copy-done.5, bf16[256,256]{1,0:T(8,128)(2,1)S(1)} %copy-done.4, bf16[256,256]{1,0:T(8,128)(2,1)S(1)} %copy-done.3, ...), custom_call_target="tpu_custom_call" | custom-call | tf_op jit(solution)/shard_map/convolve/pallas_call | solution.py:121
  59.3 0.0 copy-start.7
  59.3 0.0 copy-start.8
  59.3 32.4 %all_to_all.16 = bf16[128,8,128]{2,1,0:T(8,128)(2,1)S(1)} all-to-all(bf16[128,8,128]{2,1,0:T(8,128)(2,1)S(1)} %bitcast.13), channel_id=1, replica_groups=mesh['seq'=128,'ch'=4] {'seq'}, dimensions={0} | all-to-all | bytes 524288 | tf_op jit(solution)/shard_map/all_to_all | solution.py:156
  91.7 0.0 copy-done.10
  91.7 0.0 copy-done.11
  91.7 0.0 copy-done.12
  91.7 0.0 copy-done.7
  91.7 0.0 copy-done.8
  91.7 0.3 multiply_reduce_fusion
  92.1 11.3 %all_to_all.17 = f32[4,1,128]{2,1,0:T(1,128)S(1)} all-to-all(f32[4,1,128]{2,1,0:T(1,128)S(1)} %broadcast_in_dim.2), channel_id=1, replica_groups=mesh['seq'=128,'ch'=4] {'ch'}, dimensions={0} | all-to-all | bytes 4096 | tf_op jit(solution)/shard_map/all_to_all | solution.py:162
  103.4 1.0 multiply_convert_fusion
  (3 shorter events, 0.0 us)
Async XLA Ops:
  0.6 1.2 %copy-start.9 = (bf16[1024,128]{1,0:T(8,128)(2,1)S(1)}, bf16[1024,128]{1,0:T(8,128)(2,1)}, u32[]{:S(2)}) copy-start(bf16[1024,128]{1,0:T(8,128)(2,1)} %param.16) | copy-start | bytes 786436
  1.9 54.1 %copy-start = (bf16[256,256]{1,0:T(8,128)(2,1)S(1)}, bf16[256,256]{1,0:T(8,128)(2,1)}, u32[]{:S(2)}) copy-start(bf16[256,256]{1,0:T(8,128)(2,1)} %constant.24.clone.leave_lo_ref) | copy-start | bytes 393220
  1.9 54.1 %copy-start.1 = (bf16[256,256]{1,0:T(8,128)(2,1)S(1)}, bf16[256,256]{1,0:T(8,128)(2,1)}, u32[]{:S(2)}) copy-start(bf16[256,256]{1,0:T(8,128)(2,1)} %constant.23.clone.leave_hi_ref) | copy-start | bytes 393220
  1.9 54.1 %copy-start.2 = (bf16[256,256]{1,0:T(8,128)(2,1)S(1)}, bf16[256,256]{1,0:T(8,128)(2,1)}, u32[]{:S(2)}) copy-start(bf16[256,256]{1,0:T(8,128)(2,1)} %constant.22.clone.back_ref) | copy-start | bytes 393220
  1.9 54.1 %copy-start.3 = (bf16[256,256]{1,0:T(8,128)(2,1)S(1)}, bf16[256,256]{1,0:T(8,128)(2,1)}, u32[]{:S(2)}) copy-start(bf16[256,256]{1,0:T(8,128)(2,1)} %constant.21.clone.over_lo_ref) | copy-start | bytes 393220
  1.9 54.1 %copy-start.4 = (bf16[256,256]{1,0:T(8,128)(2,1)S(1)}, bf16[256,256]{1,0:T(8,128)(2,1)}, u32[]{:S(2)}) copy-start(bf16[256,256]{1,0:T(8,128)(2,1)} %constant.20.clone.over_hi_ref) | copy-start | bytes 393220
  2.0 54.1 %copy-start.5 = (bf16[256,256]{1,0:T(8,128)(2,1)S(1)}, bf16[256,256]{1,0:T(8,128)(2,1)}, u32[]{:S(2)}) copy-start(bf16[256,256]{1,0:T(8,128)(2,1)} %constant.19.clone.enter_ref) | copy-start | bytes 393220
  2.0 54.1 %copy-start.6 = (f32[1024]{0:T(1024)S(1)}, f32[1024]{0:T(1024)}, u32[]{:S(2)}) copy-start(f32[1024]{0:T(1024)} %param.19) | copy-start | bytes 12292
  56.1 35.6 %copy-start.10 = (bf16[1024,128]{1,0:T(8,128)(2,1)S(1)}, bf16[1024,128]{1,0:T(8,128)(2,1)}, u32[]{:S(2)}) copy-start(bf16[1024,128]{1,0:T(8,128)(2,1)} %param.13) | copy-start | bytes 786436
  56.1 35.6 %copy-start.11 = (bf16[1024,128]{1,0:T(8,128)(2,1)S(1)}, bf16[1024,128]{1,0:T(8,128)(2,1)}, u32[]{:S(2)}) copy-start(bf16[1024,128]{1,0:T(8,128)(2,1)} %param.18) | copy-start | bytes 786436
  56.1 35.6 %copy-start.12 = (f32[1024]{0:T(1024)S(1)}, f32[1024]{0:T(1024)}, u32[]{:S(2)}) copy-start(f32[1024]{0:T(1024)} %param.17) | copy-start | bytes 12292
  59.3 32.4 %copy-start.7 = (bf16[1024,128]{1,0:T(8,128)(2,1)S(1)}, bf16[1024,128]{1,0:T(8,128)(2,1)}, u32[]{:S(2)}) copy-start(bf16[1024,128]{1,0:T(8,128)(2,1)} %param.15) | copy-start | bytes 786436
  59.3 32.4 %copy-start.8 = (bf16[1024,128]{1,0:T(8,128)(2,1)S(1)}, bf16[1024,128]{1,0:T(8,128)(2,1)}, u32[]{:S(2)}) copy-start(bf16[1024,128]{1,0:T(8,128)(2,1)} %param.14) | copy-start | bytes 786436

commit v3 on v2

--- a/solution.py
+++ b/solution.py
@@ -6,6 +6,7 @@
 from jax import lax
 from jax.experimental import pallas as pl
 from jax.experimental.pallas import tpu as pltpu
+from jax.sharding import Mesh
 from jax.sharding import PartitionSpec as P
 
 D = 4096
@@ -58,8 +59,8 @@
 
 
 def convolve_kernel(
-    rows_ref, gain_ref, enter_ref, over_hi_ref, over_lo_ref, back_ref, leave_hi_ref,
-    leave_lo_ref, out_ref, kept_ref, real_ref, imag_ref, joint_hi_ref, joint_lo_ref, pair_hi_ref, pair_lo_ref,
+    core_ref, rows_ref, gain_ref, enter_ref, over_hi_ref, over_lo_ref, back_ref, leave_hi_ref,
+    leave_lo_ref, own_ref, other_ref, kept_ref, real_ref, imag_ref, joint_hi_ref, joint_lo_ref, pair_hi_ref, pair_lo_ref,
     early_ref, late_ref,
 ):
     chunk = 256
@@ -110,18 +111,34 @@
         early_ref[pl.ds(chan, BLOCKS, stride=GROUP), :] = timeline[:, :WIDTH]
         late_ref[pl.ds(GROUP + chan, BLOCKS, stride=GROUP), :] = timeline[:, WIDTH:]
     kept_ref[...] = gain_ref[...]
-    out_ref[...] = (early_ref[...] + late_ref[: GROUP * BLOCKS, :]).astype(BF16)
+    summed = (early_ref[...] + late_ref[: GROUP * BLOCKS, :]).reshape(
+        BLOCKS // 2, 2 * GROUP, WIDTH
+    )
+    even, odd = summed[:, :GROUP].astype(BF16), summed[:, GROUP:].astype(BF16)
+
+    @pl.when(core_ref[0] == 0)
+    def _():
+        own_ref[...] = even
+        other_ref[...] = odd
+
+    @pl.when(core_ref[0] != 0)
+    def _():
+        own_ref[...] = odd
+        other_ref[...] = even
 
 
 def in_vmem(value):
     return pltpu.with_memory_space_constraint(value, pltpu.VMEM)
 
 
-def convolve(rows, gain, consts):
+def convolve(core, rows, gain, consts):
     return pl.pallas_call(
         convolve_kernel,
+        in_specs=[pl.BlockSpec(memory_space=pltpu.SMEM)]
+        + [pl.BlockSpec(memory_space=pltpu.VMEM)] * (2 + len(consts)),
         out_shape=(
-            pltpu.VMEM((GROUP * BLOCKS, WIDTH), BF16),
+            pltpu.VMEM((BLOCKS // 2, GROUP, WIDTH), BF16),
+            pltpu.VMEM((BLOCKS // 2, GROUP, WIDTH), BF16),
             pltpu.VMEM(gain.shape, F32),
         ),
         scratch_shapes=[
@@ -135,26 +152,32 @@
             pltpu.VMEM((GROUP * (BLOCKS + 1), WIDTH), F32),
         ],
         name="convolve",
-    )(in_vmem(rows), in_vmem(gain), *[in_vmem(table) for table in consts])
+    )(core, in_vmem(rows), in_vmem(gain), *[in_vmem(table) for table in consts])
 
 
 def on_device(out_gate, key_proj, value_proj, long_filter, skip_gain, residual, norm_gain):
     chans, width = key_proj.shape
-    blocks = lax.axis_size("seq")
+    blocks = lax.axis_size("chip") * lax.axis_size("core")
+    core = lax.axis_index("core")
     consts = [jnp.asarray(table) for table in tables()]
     gated = lax.reduce_precision(key_proj.astype(F32) * value_proj.astype(F32), 8, 7)
     both = jnp.concatenate(
         [gated.astype(BF16).reshape(blocks, GROUP, width), long_filter.reshape(blocks, GROUP, width)],
         axis=1,
     )
-    arrived = lax.all_to_all(both, "seq", 0, 0, tiled=True)
-    convolved, gain = convolve(
+    both, core = lax.optimization_barrier((both, core.astype(jnp.int32).reshape(1)))
+    arrived = lax.all_to_all(both, ("chip", "core"), 0, 0, tiled=True)
+    own, other, gain = convolve(
+        core,
         arrived.reshape(2 * GROUP * blocks, width),
         norm_gain.reshape(chans // WIDTH, WIDTH),
         consts,
     )
-    convolved = lax.all_to_all(convolved.reshape(blocks, GROUP, width), "seq", 0, 0, tiled=True)
-    convolved = convolved.reshape(chans, width).astype(F32)
+    met = lax.ppermute(other, "core", [(0, 1), (1, 0)])
+    both = jnp.where(
+        core[0] == 0, jnp.concatenate([own, met], axis=1), jnp.concatenate([met, own], axis=1)
+    )
+    convolved = lax.all_to_all(both, "chip", 0, 0, tiled=True).reshape(chans, width).astype(F32)
     total = residual.astype(F32) + out_gate.astype(F32) * (convolved + skip_gain[:, None] * gated)
     squares = jnp.sum(total * total, axis=0, keepdims=True)
     count = lax.axis_size("ch")
@@ -169,18 +192,12 @@
 
 
 def solution(mesh):
+    mesh = Mesh(mesh.devices.reshape(BLOCKS // 2, 2, -1), ("chip", "core", "ch"))
+    wide, column = P("ch", ("chip", "core")), P("ch")
     return jax.shard_map(
         on_device,
         mesh=mesh,
-        in_specs=(
-            P("ch", "seq"),
-            P("ch", "seq"),
-            P("ch", "seq"),
-            P("ch", "seq"),
-            P("ch"),
-            P("ch", "seq"),
-            P("ch"),
-        ),
-        out_specs=(P("ch", "seq"), P("ch", "seq")),
+        in_specs=(wide, wide, wide, wide, column, wide, column),
+        out_specs=(wide, wide),
         check_vma=False,
     )

time: 105 us -> 107 us (1.019)
  starting transfers between devices: 0 us -> 2.31 us
    all_to_all x2, blocking collectives: 86.4 us -> 81.7 us  [the longest x1 54.1 us: on_device(): arrived = lax.all_to_all(both, ('chip', 'core'), 0, 0, tiled=True)]
    all_to_all x1, blocking collectives: 11.3 us -> 14.9 us  [on_device(): lax.all_to_all(jnp.broadcast_to(squares[None], (count, 1, width)), 'ch',...]
    ppermute x0 -> x1, starting transfers between devices: none -> 2.31 us  [on_device(): met = lax.ppermute(other, 'core', [(0, 1), (1, 0)])]
  transfers between devices with their start and end apart: 0 -> 1, of which waited for: 0 -> 1; matrix products, arithmetic and copies ran while one was open for 0% -> 0% of each run, Pallas kernels for 0% -> 0%
where the time goes in v3:
time: 107 us
  blocking collectives  96.7 us (90%)
  Pallas kernels  3.17 us (3%)
  other arithmetic  2.64 us (2%)
  starting transfers between devices  2.31 us (2%)
    all_to_all x1, blocking collectives, on_device(): arrived = lax.all_to_all(both, ('chip', 'core'), 0, 0, tiled=True)  54.1 us
    all_to_all x1, blocking collectives, on_device(): lax.all_to_all(both, 'chip', 0, 0, tiled=True).reshape(chans, width)  27.7 us
    all_to_all x1, blocking collectives, on_device(): lax.all_to_all(jnp.broadcast_to(squares[None], (count, 1, width)), 'ch',...  14.9 us
    pallas_call x1, Pallas kernels, convolve(): pl.pallas_call(convolve_kernel, in_specs=[pl.BlockSpec(memory_space=pltpu...  3.17 us
    ppermute x1, starting transfers between devices, on_device(): met = lax.ppermute(other, 'core', [(0, 1), (1, 0)])  2.31 us
  transfers between devices with their start and end apart: 1, of which 1 were waited for; matrix products, arithmetic and copies ran while one was open for 0% of the time, Pallas kernels for 0%

profile of v3, /device:TPU:1, one launch (start us, length us, event | category | flops | bytes accessed | tf_op | source)
XLA Modules:
  0.0 106.7 jit_solution(598254661635055618)
XLA Ops:
  0.6 0.0 copy-start.9
  0.6 1.1 %fusion.3 = bf16[128,8,128]{2,1,0:T(8,128)(2,1)S(1)} fusion(bf16[1024,128]{1,0:T(8,128)(2,1)} %param.15, bf16[1024,128]{1,0:T(8,128)(2,1)} %param.14), kind=kLoop, calls=%fused_computation.8 | loop fusion | flops 655360 | bytes 786432 | tf_op jit(solution)/shard_map/reshape | solution.py:165
  1.8 0.0 copy-done.9
  1.8 0.1 pad_maximum_fusion
  1.9 0.0 copy-start
  1.9 0.0 copy-start.1
  1.9 0.0 copy-start.2
  1.9 0.0 copy-start.3
  2.0 0.0 copy-start.4
  2.0 0.0 copy-start.5
  2.0 0.0 copy-start.6
  2.0 54.1 %all_to_all.15 = bf16[128,16,128]{2,1,0:T(8,128)(2,1)S(1)} all-to-all(bf16[128,16,128]{2,1,0:T(8,128)(2,1)S(1)} %pad_maximum_fusion), channel_id=1, replica_groups=mesh['chip'=64,'core'=2,'ch'=4] {'chip','core'}, dimensions={0} | all-to-all | bytes 1048576 | tf_op jit(solution)/shard_map/all_to_all | solution.py:169
  56.0 0.0 copy-done
  56.0 0.0 copy-done.1
  56.0 0.0 copy-done.2
  56.1 0.0 copy-done.3
  56.1 0.0 copy-done.4
  56.1 0.0 copy-done.5
  56.1 0.0 copy-done.6
  56.1 0.0 copy-start.12
  56.1 3.2 %convolve.1 = (bf16[64,8,128]{2,1,0:T(8,128)(2,1)S(1)}, bf16[64,8,128]{2,1,0:T(8,128)(2,1)S(1)}, f32[8,128]{1,0:T(8,128)S(1)}) custom-call(s32[1]{0:T(128)} %bitcast.2.core_ref, bf16[2048,128]{1,0:T(8,128)(2,1)S(1)} %bitcast.13, f32[8,128]{1,0:T(8,128)S(1)} %bitcast.14, bf16[256,256]{1,0:T(8,128)(2,1)S(1)} %copy-done, bf16[256,256]{1,0:T(8,128)(2,1)S(1)} %copy-done.1, ...), custom_call_target="tpu_custom_call" | custom-call | tf_op jit(solution)/shard_map/convolve/pallas_call | solution.py:135
  59.3 2.3 %collective-permute-start = (bf16[64,8,128]{2,1,0:T(8,128)(2,1)S(1)}, bf16[64,8,128]{2,1,0:T(8,128)(2,1)S(1)}, u32[]{:S(2)}, u32[]{:S(2)}) collective-permute-start(bf16[64,8,128]{2,1,0:T(8,128)(2,1)S(1)} %get-tuple-element.10), channel_id=1, source_target_pairs={{0,4},{4,0},{1,5},{5,1},{2,6},{6,2},{3,7},{7,3},{8,12},{12,8},{9,1... | collective-permute-start | bytes 393224 | tf_op jit(solution)/shard_map/ppermute | solution.py:176
  61.6 1.0 collective-permute-done
  62.6 0.0 copy-start.10
  62.6 0.0 copy-start.11
  62.6 0.1 maximum_select_fusion
  62.7 0.0 copy-start.7
  62.7 0.0 copy-start.8
  62.7 27.7 %all_to_all.16 = bf16[64,16,128]{2,1,0:T(8,128)(2,1)S(1)} all-to-all(bf16[64,16,128]{2,1,0:T(8,128)(2,1)S(1)} %maximum_select_fusion), channel_id=1, replica_groups=mesh['chip'=64,'core'=2,'ch'=4] {'chip'}, dimensions={0} | all-to-all | bytes 524288 | tf_op jit(solution)/shard_map/all_to_all | solution.py:180
  90.4 0.0 copy-done.12
  90.4 0.0 copy-done.10
  90.4 0.0 copy-done.11
  90.4 0.0 copy-done.7
  90.4 0.0 copy-done.8
  90.4 0.3 multiply_reduce_fusion
  90.7 14.9 %all_to_all.17 = f32[4,1,128]{2,1,0:T(1,128)S(1)} all-to-all(f32[4,1,128]{2,1,0:T(1,128)S(1)} %broadcast_in_dim.2), channel_id=1, replica_groups=mesh['chip'=64,'core'=2,'ch'=4] {'ch'}, dimensions={0} | all-to-all | bytes 4096 | tf_op jit(solution)/shard_map/all_to_all | solution.py:185
  105.7 1.0 multiply_convert_fusion
  (3 shorter events, 0.0 us)
Async XLA Ops:
  0.6 1.2 %copy-start.9 = (bf16[1024,128]{1,0:T(8,128)(2,1)S(1)}, bf16[1024,128]{1,0:T(8,128)(2,1)}, u32[]{:S(2)}) copy-start(bf16[1024,128]{1,0:T(8,128)(2,1)} %param.16) | copy-start | bytes 786436
  1.9 54.1 %copy-start = (bf16[256,256]{1,0:T(8,128)(2,1)S(1)}, bf16[256,256]{1,0:T(8,128)(2,1)}, u32[]{:S(2)}) copy-start(bf16[256,256]{1,0:T(8,128)(2,1)} %constant.28.clone.enter_ref) | copy-start | bytes 393220
  1.9 54.1 %copy-start.1 = (bf16[256,256]{1,0:T(8,128)(2,1)S(1)}, bf16[256,256]{1,0:T(8,128)(2,1)}, u32[]{:S(2)}) copy-start(bf16[256,256]{1,0:T(8,128)(2,1)} %constant.29.clone.over_hi_ref) | copy-start | bytes 393220
  1.9 54.1 %copy-start.2 = (bf16[256,256]{1,0:T(8,128)(2,1)S(1)}, bf16[256,256]{1,0:T(8,128)(2,1)}, u32[]{:S(2)}) copy-start(bf16[256,256]{1,0:T(8,128)(2,1)} %constant.30.clone.over_lo_ref) | copy-start | bytes 393220
  1.9 54.1 %copy-start.3 = (bf16[256,256]{1,0:T(8,128)(2,1)S(1)}, bf16[256,256]{1,0:T(8,128)(2,1)}, u32[]{:S(2)}) copy-start(bf16[256,256]{1,0:T(8,128)(2,1)} %constant.31.clone.back_ref) | copy-start | bytes 393220
  2.0 54.1 %copy-start.4 = (bf16[256,256]{1,0:T(8,128)(2,1)S(1)}, bf16[256,256]{1,0:T(8,128)(2,1)}, u32[]{:S(2)}) copy-start(bf16[256,256]{1,0:T(8,128)(2,1)} %constant.32.clone.leave_hi_ref) | copy-start | bytes 393220
  2.0 54.1 %copy-start.5 = (bf16[256,256]{1,0:T(8,128)(2,1)S(1)}, bf16[256,256]{1,0:T(8,128)(2,1)}, u32[]{:S(2)}) copy-start(bf16[256,256]{1,0:T(8,128)(2,1)} %constant.33.clone.leave_lo_ref) | copy-start | bytes 393220
  2.0 54.1 %copy-start.6 = (f32[1024]{0:T(1024)S(1)}, f32[1024]{0:T(1024)}, u32[]{:S(2)}) copy-start(f32[1024]{0:T(1024)} %param.19) | copy-start | bytes 12292
  56.1 34.3 %copy-start.12 = (f32[1024]{0:T(1024)S(1)}, f32[1024]{0:T(1024)}, u32[]{:S(2)}) copy-start(f32[1024]{0:T(1024)} %param.17) | copy-start | bytes 12292
  59.3 3.3 %collective-permute-start = (bf16[64,8,128]{2,1,0:T(8,128)(2,1)S(1)}, bf16[64,8,128]{2,1,0:T(8,128)(2,1)S(1)}, u32[]{:S(2)}, u32[]{:S(2)}) collective-permute-start(bf16[64,8,128]{2,1,0:T(8,128)(2,1)S(1)} %get-tuple-element.10), channel_id=1, source_target_pairs={{0,4},{4,0},{1,5},{5,1},{2,6},{6,2},{3,7},{7,3},{8,12},{12,8},{9,1... | collective-permute-start | bytes 393224 | tf_op jit(solution)/shard_map/ppermute | solution.py:176
  62.6 27.8 %copy-start.10 = (bf16[1024,128]{1,0:T(8,128)(2,1)S(1)}, bf16[1024,128]{1,0:T(8,128)(2,1)}, u32[]{:S(2)}) copy-start(bf16[1024,128]{1,0:T(8,128)(2,1)} %param.13) | copy-start | bytes 786436
  62.6 27.8 %copy-start.11 = (bf16[1024,128]{1,0:T(8,128)(2,1)S(1)}, bf16[1024,128]{1,0:T(8,128)(2,1)}, u32[]{:S(2)}) copy-start(bf16[1024,128]{1,0:T(8,128)(2,1)} %param.18) | copy-start | bytes 786436
  62.7 27.7 %copy-start.7 = (bf16[1024,128]{1,0:T(8,128)(2,1)S(1)}, bf16[1024,128]{1,0:T(8,128)(2,1)}, u32[]{:S(2)}) copy-start(bf16[1024,128]{1,0:T(8,128)(2,1)} %param.15) | copy-start | bytes 786436
  62.7 27.7 %copy-start.8 = (bf16[1024,128]{1,0:T(8,128)(2,1)S(1)}, bf16[1024,128]{1,0:T(8,128)(2,1)}, u32[]{:S(2)}) copy-start(bf16[1024,128]{1,0:T(8,128)(2,1)} %param.14) | copy-start | bytes 786436

commit v4 on v2

--- a/solution.py
+++ b/solution.py
@@ -59,18 +59,25 @@
 
 def convolve_kernel(
     rows_ref, gain_ref, enter_ref, over_hi_ref, over_lo_ref, back_ref, leave_hi_ref,
-    leave_lo_ref, out_ref, kept_ref, real_ref, imag_ref, joint_hi_ref, joint_lo_ref, pair_hi_ref, pair_lo_ref,
+    leave_lo_ref, out_ref, kept_ref, in_re_ref, in_im_ref, lag_re_ref, lag_im_ref,
+    joint_hi_ref, joint_lo_ref, pair_hi_ref, pair_lo_ref,
     early_ref, late_ref,
 ):
-    chunk = 256
+    chunk = 512
     for start in range(0, 2 * GROUP * BLOCKS, chunk):
         piece = rows_ref[start : start + chunk, :]
         spectrum = dot(jnp.concatenate([piece, piece], axis=1), enter_ref[...])
-        real_ref[start : start + chunk, :] = spectrum[:, :WIDTH]
-        imag_ref[start : start + chunk, :] = spectrum[:, WIDTH:]
+        spectrum = spectrum.reshape(chunk // (2 * GROUP), 2 * GROUP, SPAN)
+        signal = spectrum[:, :GROUP].reshape(chunk // 2, SPAN)
+        lags = spectrum[:, GROUP:].reshape(chunk // 2, SPAN)
+        rows = pl.ds(start // 2, chunk // 2)
+        in_re_ref[rows, :] = signal[:, :WIDTH]
+        in_im_ref[rows, :] = signal[:, WIDTH:]
+        lag_re_ref[rows, :] = lags[:, :WIDTH]
+        lag_im_ref[rows, :] = lags[:, WIDTH:]
 
-    def over_blocks(row):
-        rows = pl.ds(row, BLOCKS, stride=2 * GROUP)
+    def over_blocks(real_ref, imag_ref, chan):
+        rows = pl.ds(chan, BLOCKS, stride=GROUP)
         high, low = halves(jnp.concatenate([real_ref[rows, :], imag_ref[rows, :]], axis=1))
         both = jnp.concatenate([high, low], axis=0)
         sums = dot(over_hi_ref[...], both) + dot(over_lo_ref[...], both)
@@ -79,8 +86,8 @@
         return cos_re + sin_im, cos_im - sin_re, cos_re - sin_im, cos_im + sin_re
 
     for chan in range(GROUP):
-        xp_re, xp_im, xm_re, xm_im = over_blocks(chan)
-        hp_re, hp_im, hm_re, hm_im = over_blocks(GROUP + chan)
+        xp_re, xp_im, xm_re, xm_im = over_blocks(in_re_ref, in_im_ref, chan)
+        hp_re, hp_im, hm_re, hm_im = over_blocks(lag_re_ref, lag_im_ref, chan)
         pp_re = xp_re * hp_re - xp_im * hp_im
         pp_im = xp_re * hp_im + xp_im * hp_re
         pm_re = xm_re * hm_re - xm_im * hm_im
@@ -125,8 +132,10 @@
             pltpu.VMEM(gain.shape, F32),
         ),
         scratch_shapes=[
-            pltpu.VMEM((2 * GROUP * BLOCKS, WIDTH), F32),
-            pltpu.VMEM((2 * GROUP * BLOCKS, WIDTH), F32),
+            pltpu.VMEM((GROUP * BLOCKS, WIDTH), F32),
+            pltpu.VMEM((GROUP * BLOCKS, WIDTH), F32),
+            pltpu.VMEM((GROUP * BLOCKS, WIDTH), F32),
+            pltpu.VMEM((GROUP * BLOCKS, WIDTH), F32),
             pltpu.VMEM((GROUP * SPAN, SPAN), BF16),
             pltpu.VMEM((GROUP * SPAN, SPAN), BF16),
             pltpu.VMEM((GROUP * BLOCKS, SPAN), BF16),
@@ -157,13 +166,7 @@
     convolved = convolved.reshape(chans, width).astype(F32)
     total = residual.astype(F32) + out_gate.astype(F32) * (convolved + skip_gain[:, None] * gated)
     squares = jnp.sum(total * total, axis=0, keepdims=True)
-    count = lax.axis_size("ch")
-    squares = jnp.sum(
-        lax.all_to_all(
-            jnp.broadcast_to(squares[None], (count, 1, width)), "ch", 0, 0, tiled=True
-        ),
-        axis=0,
-    )
+    squares = jnp.sum(lax.all_gather(squares, "ch"), axis=0)
     normed = total * lax.rsqrt(squares / D + 1e-06) * gain.reshape(chans)[:, None]
     return (total.astype(BF16), normed.astype(BF16))
 

time: 105 us -> 104 us (level)
    all_to_all x1 -> x0, blocking collectives: 11.3 us -> none  [on_device(): lax.all_to_all(jnp.broadcast_to(squares[None], (count, 1, width)), 'ch',...]
    all_gather x0 -> x1, blocking collectives: none -> 10.9 us  [on_device(): squares = jnp.sum(lax.all_gather(squares, 'ch'), axis=0)]
where the time goes in v4:
time: 104 us
  blocking collectives  97.1 us (93%)
  Pallas kernels  2.98 us (3%)
  other arithmetic  2.57 us (2%)
    all_to_all x1, blocking collectives, on_device(): arrived = lax.all_to_all(both, 'seq', 0, 0, tiled=True)  54.1 us
    all_to_all x1, blocking collectives, on_device(): lax.all_to_all(convolved.reshape(blocks, GROUP, width), 'seq', 0, 0, tile...  32.1 us
    all_gather x1, blocking collectives, on_device(): squares = jnp.sum(lax.all_gather(squares, 'ch'), axis=0)  10.9 us
    pallas_call x1, Pallas kernels, convolve(): pl.pallas_call(convolve_kernel, out_shape=(pltpu.VMEM((GROUP * BLOCKS, WI...  2.98 us

profile of v4, /device:TPU:1, one launch (start us, length us, event | category | flops | bytes accessed | tf_op | source)
XLA Modules:
  0.0 103.5 jit_solution(7255768811218361425)
XLA Ops:
  0.6 0.0 copy-start.9
  0.6 1.1 %fusion.3 = bf16[128,8,128]{2,1,0:T(8,128)(2,1)S(1)} fusion(bf16[1024,128]{1,0:T(8,128)(2,1)} %param.15, bf16[1024,128]{1,0:T(8,128)(2,1)} %param.14), kind=kLoop, calls=%fused_computation.8 | loop fusion | flops 655360 | bytes 786432 | tf_op jit(solution)/shard_map/reshape | solution.py:156
  1.8 0.0 copy-done.9
  1.8 0.1 pad_maximum_fusion
  1.9 0.0 copy-start
  1.9 0.0 copy-start.1
  1.9 0.0 copy-start.2
  1.9 0.0 copy-start.3
  1.9 0.0 copy-start.4
  2.0 0.0 copy-start.5
  2.0 0.0 copy-start.6
  2.0 54.1 %all_to_all.10 = bf16[128,16,128]{2,1,0:T(8,128)(2,1)S(1)} all-to-all(bf16[128,16,128]{2,1,0:T(8,128)(2,1)S(1)} %pad_maximum_fusion), channel_id=1, replica_groups=mesh['seq'=128,'ch'=4] {'seq'}, dimensions={0} | all-to-all | bytes 1048576 | tf_op jit(solution)/shard_map/all_to_all | solution.py:159
  56.0 0.0 copy-done
  56.0 0.0 copy-done.1
  56.0 0.0 copy-done.2
  56.0 0.0 copy-done.3
  56.1 0.0 copy-done.4
  56.1 0.0 copy-done.5
  56.1 0.0 copy-done.6
  56.1 0.0 copy-start.10
  56.1 0.0 copy-start.11
  56.1 0.0 copy-start.12
  56.1 3.0 %convolve.1 = (bf16[1024,128]{1,0:T(8,128)(2,1)S(1)}, f32[8,128]{1,0:T(8,128)S(1)}) custom-call(bf16[2048,128]{1,0:T(8,128)(2,1)S(1)} %bitcast.12, f32[8,128]{1,0:T(8,128)S(1)} %bitcast.14, bf16[256,256]{1,0:T(8,128)(2,1)S(1)} %copy-done.5, bf16[256,256]{1,0:T(8,128)(2,1)S(1)} %copy-done.4, bf16[256,256]{1,0:T(8,128)(2,1)S(1)} %copy-done.3, ...), custom_call_target="tpu_custom_call" | custom-call | tf_op jit(solution)/shard_map/convolve/pallas_call | solution.py:128
  59.1 0.0 copy-start.7
  59.1 0.0 copy-start.8
  59.1 32.1 %all_to_all.11 = bf16[128,8,128]{2,1,0:T(8,128)(2,1)S(1)} all-to-all(bf16[128,8,128]{2,1,0:T(8,128)(2,1)S(1)} %bitcast.13), channel_id=1, replica_groups=mesh['seq'=128,'ch'=4] {'seq'}, dimensions={0} | all-to-all | bytes 524288 | tf_op jit(solution)/shard_map/all_to_all | solution.py:165
  91.3 0.0 copy-done.10
  91.3 0.0 copy-done.11
  91.3 0.0 copy-done.12
  91.3 0.0 copy-done.7
  91.3 0.0 copy-done.8
  91.3 0.3 multiply_reduce_fusion
  91.6 10.9 %all-gather.1 = f32[4,1,128]{2,1,0:T(1,128)S(1)} all-gather(f32[1,1,128]{2,1,0:T(1,128)S(1)} %bitcast.17), channel_id=2, replica_groups=mesh['seq'=128,'ch'=4] {'ch'}, dimensions={0}, use_global_device_ids=true | all-gather | bytes 2560 | tf_op jit(solution)/shard_map/all_gather | solution.py:169
  102.6 1.0 multiply_convert_fusion
  (2 shorter events, 0.0 us)
Async XLA Ops:
  0.6 1.2 %copy-start.9 = (bf16[1024,128]{1,0:T(8,128)(2,1)S(1)}, bf16[1024,128]{1,0:T(8,128)(2,1)}, u32[]{:S(2)}) copy-start(bf16[1024,128]{1,0:T(8,128)(2,1)} %param.16) | copy-start | bytes 786436
  1.9 54.1 %copy-start = (bf16[256,256]{1,0:T(8,128)(2,1)S(1)}, bf16[256,256]{1,0:T(8,128)(2,1)}, u32[]{:S(2)}) copy-start(bf16[256,256]{1,0:T(8,128)(2,1)} %constant.24.clone.leave_lo_ref) | copy-start | bytes 393220
  1.9 54.1 %copy-start.1 = (bf16[256,256]{1,0:T(8,128)(2,1)S(1)}, bf16[256,256]{1,0:T(8,128)(2,1)}, u32[]{:S(2)}) copy-start(bf16[256,256]{1,0:T(8,128)(2,1)} %constant.23.clone.leave_hi_ref) | copy-start | bytes 393220
  1.9 54.1 %copy-start.2 = (bf16[256,256]{1,0:T(8,128)(2,1)S(1)}, bf16[256,256]{1,0:T(8,128)(2,1)}, u32[]{:S(2)}) copy-start(bf16[256,256]{1,0:T(8,128)(2,1)} %constant.22.clone.back_ref) | copy-start | bytes 393220
  1.9 54.1 %copy-start.3 = (bf16[256,256]{1,0:T(8,128)(2,1)S(1)}, bf16[256,256]{1,0:T(8,128)(2,1)}, u32[]{:S(2)}) copy-start(bf16[256,256]{1,0:T(8,128)(2,1)} %constant.21.clone.over_lo_ref) | copy-start | bytes 393220
  1.9 54.1 %copy-start.4 = (bf16[256,256]{1,0:T(8,128)(2,1)S(1)}, bf16[256,256]{1,0:T(8,128)(2,1)}, u32[]{:S(2)}) copy-start(bf16[256,256]{1,0:T(8,128)(2,1)} %constant.20.clone.over_hi_ref) | copy-start | bytes 393220
  2.0 54.1 %copy-start.5 = (bf16[256,256]{1,0:T(8,128)(2,1)S(1)}, bf16[256,256]{1,0:T(8,128)(2,1)}, u32[]{:S(2)}) copy-start(bf16[256,256]{1,0:T(8,128)(2,1)} %constant.19.clone.enter_ref) | copy-start | bytes 393220
  2.0 54.1 %copy-start.6 = (f32[1024]{0:T(1024)S(1)}, f32[1024]{0:T(1024)}, u32[]{:S(2)}) copy-start(f32[1024]{0:T(1024)} %param.19) | copy-start | bytes 12292
  56.1 35.2 %copy-start.10 = (bf16[1024,128]{1,0:T(8,128)(2,1)S(1)}, bf16[1024,128]{1,0:T(8,128)(2,1)}, u32[]{:S(2)}) copy-start(bf16[1024,128]{1,0:T(8,128)(2,1)} %param.13) | copy-start | bytes 786436
  56.1 35.2 %copy-start.11 = (bf16[1024,128]{1,0:T(8,128)(2,1)S(1)}, bf16[1024,128]{1,0:T(8,128)(2,1)}, u32[]{:S(2)}) copy-start(bf16[1024,128]{1,0:T(8,128)(2,1)} %param.18) | copy-start | bytes 786436
  56.1 35.2 %copy-start.12 = (f32[1024]{0:T(1024)S(1)}, f32[1024]{0:T(1024)}, u32[]{:S(2)}) copy-start(f32[1024]{0:T(1024)} %param.17) | copy-start | bytes 12292
  59.1 32.2 %copy-start.7 = (bf16[1024,128]{1,0:T(8,128)(2,1)S(1)}, bf16[1024,128]{1,0:T(8,128)(2,1)}, u32[]{:S(2)}) copy-start(bf16[1024,128]{1,0:T(8,128)(2,1)} %param.15) | copy-start | bytes 786436
  59.1 32.2 %copy-start.8 = (bf16[1024,128]{1,0:T(8,128)(2,1)S(1)}, bf16[1024,128]{1,0:T(8,128)(2,1)}, u32[]{:S(2)}) copy-start(bf16[1024,128]{1,0:T(8,128)(2,1)} %param.14) | copy-start | bytes 786436

commit v5 on v4

--- a/solution.py
+++ b/solution.py
@@ -12,10 +12,18 @@
 BLOCKS = 128
 WIDTH = 128
 GROUP = 8
+LEAD = 85
+CH_LEAD = 1
 SPAN = 256
 
 F32 = jnp.float32
 BF16 = jnp.bfloat16
+
+
+def led_by(first, count):
+    order = list(range(count))
+    order[0], order[first] = first, 0
+    return order
 
 
 def split_table(table):
@@ -34,7 +42,8 @@
     enter = np.concatenate([np.cos(phase), -np.sin(phase)], axis=1)
     enter = np.concatenate(split_table(enter), axis=0)
 
-    phase = angles(steps[:, None], steps[None, :])
+    arrival = np.array(led_by(LEAD, BLOCKS))
+    phase = angles(steps[:, None], arrival[None, :])
     over = np.concatenate([np.cos(phase), np.sin(phase)], axis=0)
     over_hi, over_lo = (np.concatenate([part, part], axis=1) for part in split_table(over))
 
@@ -117,7 +126,17 @@
         early_ref[pl.ds(chan, BLOCKS, stride=GROUP), :] = timeline[:, :WIDTH]
         late_ref[pl.ds(GROUP + chan, BLOCKS, stride=GROUP), :] = timeline[:, WIDTH:]
     kept_ref[...] = gain_ref[...]
-    out_ref[...] = (early_ref[...] + late_ref[: GROUP * BLOCKS, :]).astype(BF16)
+    summed = early_ref[...] + late_ref[: GROUP * BLOCKS, :]
+    lead = LEAD * GROUP
+    out_ref[...] = jnp.concatenate(
+        [
+            summed[lead : lead + GROUP],
+            summed[GROUP:lead],
+            summed[:GROUP],
+            summed[lead + GROUP :],
+        ],
+        axis=0,
+    ).astype(BF16)
 
 
 def in_vmem(value):
@@ -156,17 +175,26 @@
         [gated.astype(BF16).reshape(blocks, GROUP, width), long_filter.reshape(blocks, GROUP, width)],
         axis=1,
     )
-    arrived = lax.all_to_all(both, "seq", 0, 0, tiled=True)
+    members = [led_by(LEAD, blocks)]
+    arrived = lax.all_to_all(both, "seq", 0, 0, axis_index_groups=members, tiled=True)
     convolved, gain = convolve(
         arrived.reshape(2 * GROUP * blocks, width),
         norm_gain.reshape(chans // WIDTH, WIDTH),
         consts,
     )
-    convolved = lax.all_to_all(convolved.reshape(blocks, GROUP, width), "seq", 0, 0, tiled=True)
+    convolved = lax.all_to_all(
+        convolved.reshape(blocks, GROUP, width),
+        "seq",
+        0,
+        0,
+        axis_index_groups=members,
+        tiled=True,
+    )
     convolved = convolved.reshape(chans, width).astype(F32)
     total = residual.astype(F32) + out_gate.astype(F32) * (convolved + skip_gain[:, None] * gated)
     squares = jnp.sum(total * total, axis=0, keepdims=True)
-    squares = jnp.sum(lax.all_gather(squares, "ch"), axis=0)
+    owners = [led_by(CH_LEAD, lax.axis_size("ch"))]
+    squares = jnp.sum(lax.all_gather(squares, "ch", axis_index_groups=owners), axis=0)
     normed = total * lax.rsqrt(squares / D + 1e-06) * gain.reshape(chans)[:, None]
     return (total.astype(BF16), normed.astype(BF16))
 

time: 104 us -> 92.2 us (0.89)
  blocking collectives: 97.1 us -> 84.7 us
    all_to_all x2, blocking collectives: 86.2 us -> 74 us  [the longest x1 48.2 us: on_device(): lax.all_to_all(both, 'seq', 0, 0, axis_index_groups=members, tiled=True)]
where the time goes in v5:
time: 92.2 us; the launch traced here: 91.2 us
  blocking collectives  84.7 us (92%)
  Pallas kernels  2.98 us (3%)
  other arithmetic  2.57 us (3%)
    all_to_all x1, blocking collectives, on_device(): lax.all_to_all(both, 'seq', 0, 0, axis_index_groups=members, tiled=True)  48.2 us
    all_to_all x1, blocking collectives, on_device(): lax.all_to_all(convolved.reshape(blocks, GROUP, width), 'seq', 0, 0, axis...  25.9 us
    all_gather x1, blocking collectives, on_device(): lax.all_gather(squares, 'ch', axis_index_groups=owners)  10.7 us
    pallas_call x1, Pallas kernels, convolve(): pl.pallas_call(convolve_kernel, out_shape=(pltpu.VMEM((GROUP * BLOCKS, WI...  2.98 us

profile of v5, /device:TPU:1, one launch (start us, length us, event | category | flops | bytes accessed | tf_op | source)
XLA Modules:
  0.0 91.2 jit_solution(13272560818235650950)
XLA Ops:
  0.6 0.0 copy-start.9
  0.6 1.1 %fusion.3 = bf16[128,8,128]{2,1,0:T(8,128)(2,1)S(1)} fusion(bf16[1024,128]{1,0:T(8,128)(2,1)} %param.15, bf16[1024,128]{1,0:T(8,128)(2,1)} %param.14), kind=kLoop, calls=%fused_computation.8 | loop fusion | flops 655360 | bytes 786432 | tf_op jit(solution)/shard_map/reshape | solution.py:175
  1.8 0.0 copy-done.9
  1.8 0.1 pad_maximum_fusion
  1.9 0.0 copy-start
  1.9 0.0 copy-start.1
  1.9 0.0 copy-start.2
  1.9 0.0 copy-start.3
  1.9 0.0 copy-start.4
  2.0 0.0 copy-start.5
  2.0 0.0 copy-start.6
  2.0 48.2 %all_to_all.10 = bf16[128,16,128]{2,1,0:T(8,128)(2,1)S(1)} all-to-all(bf16[128,16,128]{2,1,0:T(8,128)(2,1)S(1)} %pad_maximum_fusion), channel_id=1, replica_groups={{340,4,8,12,16,20,24,28,32,36,40,44,48,52,56,60,64,68,72,76,80,84,88,92..., dimensions={0} | all-to-all | bytes 1048576 | tf_op jit(solution)/shard_map/all_to_all | solution.py:179
  50.2 0.0 copy-done
  50.2 0.0 copy-done.1
  50.2 0.0 copy-done.2
  50.2 0.0 copy-done.3
  50.2 0.0 copy-done.4
  50.2 0.0 copy-done.5
  50.2 0.0 copy-done.6
  50.2 0.0 copy-start.10
  50.2 0.0 copy-start.11
  50.2 0.0 copy-start.12
  50.3 3.0 %convolve.1 = (bf16[1024,128]{1,0:T(8,128)(2,1)S(1)}, f32[8,128]{1,0:T(8,128)S(1)}) custom-call(bf16[2048,128]{1,0:T(8,128)(2,1)S(1)} %bitcast.12, f32[8,128]{1,0:T(8,128)S(1)} %bitcast.14, bf16[256,256]{1,0:T(8,128)(2,1)S(1)} %copy-done.5, bf16[256,256]{1,0:T(8,128)(2,1)S(1)} %copy-done.4, bf16[256,256]{1,0:T(8,128)(2,1)S(1)} %copy-done.3, ...), custom_call_target="tpu_custom_call" | custom-call | tf_op jit(solution)/shard_map/convolve/pallas_call | solution.py:147
  53.2 0.0 copy-start.7
  53.3 0.0 copy-start.8
  53.3 25.9 %all_to_all.11 = bf16[128,8,128]{2,1,0:T(8,128)(2,1)S(1)} all-to-all(bf16[128,8,128]{2,1,0:T(8,128)(2,1)S(1)} %bitcast.13), channel_id=1, replica_groups={{340,4,8,12,16,20,24,28,32,36,40,44,48,52,56,60,64,68,72,76,80,84,88,92..., dimensions={0} | all-to-all | bytes 524288 | tf_op jit(solution)/shard_map/all_to_all | solution.py:185
  79.1 0.0 copy-done.10
  79.1 0.0 copy-done.11
  79.1 0.0 copy-done.12
  79.1 0.0 copy-done.7
  79.1 0.0 copy-done.8
  79.2 0.3 multiply_reduce_fusion
  79.5 10.7 %all-gather.1 = f32[4,1,128]{2,1,0:T(1,128)S(1)} all-gather(f32[1,1,128]{2,1,0:T(1,128)S(1)} %bitcast.17), channel_id=2, replica_groups={{1,0,2,3},{5,4,6,7},{9,8,10,11},{13,12,14,15},{17,16,18,19},{21,20,22,2..., dimensions={0}, use_global_device_ids=true | all-gather | bytes 2560 | tf_op jit(solution)/shard_map/all_gather | solution.py:197
  90.2 1.0 %multiply_convert_fusion = (bf16[1024,128]{1,0:T(8,128)(2,1)}, bf16[1024,128]{1,0:T(8,128)(2,1)}) fusion(f32[1024,128]{1,0:T(8,128)S(1)} %get-tuple-element.7, f32[1024]{0:T(1024)S(1)} %bitcast.15, f32[128]{0:T(128)S(1)} %add_rsqrt_fusion), kind=kLoop, calls=%fused_computation.4 | loop fusion | flops 524288 | bytes 1053184 | tf_op jit(solution)/shard_map/convert_element_type | solution.py:199
  (2 shorter events, 0.0 us)
Async XLA Ops:
  0.6 1.2 %copy-start.9 = (bf16[1024,128]{1,0:T(8,128)(2,1)S(1)}, bf16[1024,128]{1,0:T(8,128)(2,1)}, u32[]{:S(2)}) copy-start(bf16[1024,128]{1,0:T(8,128)(2,1)} %param.16) | copy-start | bytes 786436
  1.9 48.3 %copy-start = (bf16[256,256]{1,0:T(8,128)(2,1)S(1)}, bf16[256,256]{1,0:T(8,128)(2,1)}, u32[]{:S(2)}) copy-start(bf16[256,256]{1,0:T(8,128)(2,1)} %constant.24.clone.leave_lo_ref) | copy-start | bytes 393220
  1.9 48.3 %copy-start.1 = (bf16[256,256]{1,0:T(8,128)(2,1)S(1)}, bf16[256,256]{1,0:T(8,128)(2,1)}, u32[]{:S(2)}) copy-start(bf16[256,256]{1,0:T(8,128)(2,1)} %constant.23.clone.leave_hi_ref) | copy-start | bytes 393220
  1.9 48.3 %copy-start.2 = (bf16[256,256]{1,0:T(8,128)(2,1)S(1)}, bf16[256,256]{1,0:T(8,128)(2,1)}, u32[]{:S(2)}) copy-start(bf16[256,256]{1,0:T(8,128)(2,1)} %constant.22.clone.back_ref) | copy-start | bytes 393220
  1.9 48.3 %copy-start.3 = (bf16[256,256]{1,0:T(8,128)(2,1)S(1)}, bf16[256,256]{1,0:T(8,128)(2,1)}, u32[]{:S(2)}) copy-start(bf16[256,256]{1,0:T(8,128)(2,1)} %constant.21.clone.over_lo_ref) | copy-start | bytes 393220
  1.9 48.2 %copy-start.4 = (bf16[256,256]{1,0:T(8,128)(2,1)S(1)}, bf16[256,256]{1,0:T(8,128)(2,1)}, u32[]{:S(2)}) copy-start(bf16[256,256]{1,0:T(8,128)(2,1)} %constant.20.clone.over_hi_ref) | copy-start | bytes 393220
  2.0 48.2 %copy-start.5 = (bf16[256,256]{1,0:T(8,128)(2,1)S(1)}, bf16[256,256]{1,0:T(8,128)(2,1)}, u32[]{:S(2)}) copy-start(bf16[256,256]{1,0:T(8,128)(2,1)} %constant.19.clone.enter_ref) | copy-start | bytes 393220
  2.0 48.2 %copy-start.6 = (f32[1024]{0:T(1024)S(1)}, f32[1024]{0:T(1024)}, u32[]{:S(2)}) copy-start(f32[1024]{0:T(1024)} %param.19) | copy-start | bytes 12292
  50.2 28.9 %copy-start.10 = (bf16[1024,128]{1,0:T(8,128)(2,1)S(1)}, bf16[1024,128]{1,0:T(8,128)(2,1)}, u32[]{:S(2)}) copy-start(bf16[1024,128]{1,0:T(8,128)(2,1)} %param.13) | copy-start | bytes 786436
  50.2 28.9 %copy-start.11 = (bf16[1024,128]{1,0:T(8,128)(2,1)S(1)}, bf16[1024,128]{1,0:T(8,128)(2,1)}, u32[]{:S(2)}) copy-start(bf16[1024,128]{1,0:T(8,128)(2,1)} %param.18) | copy-start | bytes 786436
  50.2 28.9 %copy-start.12 = (f32[1024]{0:T(1024)S(1)}, f32[1024]{0:T(1024)}, u32[]{:S(2)}) copy-start(f32[1024]{0:T(1024)} %param.17) | copy-start | bytes 12292
  53.2 25.9 %copy-start.7 = (bf16[1024,128]{1,0:T(8,128)(2,1)S(1)}, bf16[1024,128]{1,0:T(8,128)(2,1)}, u32[]{:S(2)}) copy-start(bf16[1024,128]{1,0:T(8,128)(2,1)} %param.15) | copy-start | bytes 786436
  53.3 25.9 %copy-start.8 = (bf16[1024,128]{1,0:T(8,128)(2,1)S(1)}, bf16[1024,128]{1,0:T(8,128)(2,1)}, u32[]{:S(2)}) copy-start(bf16[1024,128]{1,0:T(8,128)(2,1)} %param.14) | copy-start | bytes 786436

commit v6 on v5

--- a/solution.py
+++ b/solution.py
@@ -13,7 +13,7 @@
 WIDTH = 128
 GROUP = 8
 LEAD = 85
-CH_LEAD = 1
+CH_LEAD = 2
 SPAN = 256
 
 F32 = jnp.float32
@@ -193,8 +193,18 @@
     convolved = convolved.reshape(chans, width).astype(F32)
     total = residual.astype(F32) + out_gate.astype(F32) * (convolved + skip_gain[:, None] * gated)
     squares = jnp.sum(total * total, axis=0, keepdims=True)
-    owners = [led_by(CH_LEAD, lax.axis_size("ch"))]
-    squares = jnp.sum(lax.all_gather(squares, "ch", axis_index_groups=owners), axis=0)
+    count = lax.axis_size("ch")
+    squares = jnp.sum(
+        lax.all_to_all(
+            jnp.broadcast_to(squares[None], (count, 1, width)),
+            "ch",
+            0,
+            0,
+            axis_index_groups=[led_by(CH_LEAD, count)],
+            tiled=True,
+        ),
+        axis=0,
+    )
     normed = total * lax.rsqrt(squares / D + 1e-06) * gain.reshape(chans)[:, None]
     return (total.astype(BF16), normed.astype(BF16))
 

time: 92.2 us -> 91.3 us (level)
    all_gather x1 -> x0, blocking collectives: 10.7 us -> none  [on_device(): lax.all_gather(squares, 'ch', axis_index_groups=owners)]
    all_to_all x0 -> x1, blocking collectives: none -> 10.6 us  [on_device(): lax.all_to_all(jnp.broadcast_to(squares[None], (count, 1, width)), 'ch',...]
where the time goes in v6:
time: 91.3 us; the launch traced here: 91.1 us
  blocking collectives  84.6 us (93%)
  Pallas kernels  2.98 us (3%)
  other arithmetic  2.56 us (3%)
    all_to_all x1, blocking collectives, on_device(): lax.all_to_all(both, 'seq', 0, 0, axis_index_groups=members, tiled=True)  48.2 us
    all_to_all x1, blocking collectives, on_device(): lax.all_to_all(convolved.reshape(blocks, GROUP, width), 'seq', 0, 0, axis...  25.9 us
    all_to_all x1, blocking collectives, on_device(): lax.all_to_all(jnp.broadcast_to(squares[None], (count, 1, width)), 'ch',...  10.6 us
    pallas_call x1, Pallas kernels, convolve(): pl.pallas_call(convolve_kernel, out_shape=(pltpu.VMEM((GROUP * BLOCKS, WI...  2.98 us

profile of v6, /device:TPU:1, one launch (start us, length us, event | category | flops | bytes accessed | tf_op | source)
XLA Modules:
  0.0 91.1 jit_solution(6123698855323874179)
XLA Ops:
  0.6 0.0 copy-start.9
  0.6 1.1 %fusion.3 = bf16[128,8,128]{2,1,0:T(8,128)(2,1)S(1)} fusion(bf16[1024,128]{1,0:T(8,128)(2,1)} %param.15, bf16[1024,128]{1,0:T(8,128)(2,1)} %param.14), kind=kLoop, calls=%fused_computation.8 | loop fusion | flops 655360 | bytes 786432 | tf_op jit(solution)/shard_map/reshape | solution.py:175
  1.8 0.0 copy-done.9
  1.8 0.1 pad_maximum_fusion
  1.9 0.0 copy-start
  1.9 0.0 copy-start.1
  1.9 0.0 copy-start.2
  1.9 0.0 copy-start.3
  1.9 0.0 copy-start.4
  2.0 0.0 copy-start.5
  2.0 0.0 copy-start.6
  2.0 48.2 %all_to_all.15 = bf16[128,16,128]{2,1,0:T(8,128)(2,1)S(1)} all-to-all(bf16[128,16,128]{2,1,0:T(8,128)(2,1)S(1)} %pad_maximum_fusion), channel_id=1, replica_groups={{340,4,8,12,16,20,24,28,32,36,40,44,48,52,56,60,64,68,72,76,80,84,88,92..., dimensions={0} | all-to-all | bytes 1048576 | tf_op jit(solution)/shard_map/all_to_all | solution.py:179
  50.2 0.0 copy-done
  50.2 0.0 copy-done.1
  50.2 0.0 copy-done.2
  50.2 0.0 copy-done.3
  50.2 0.0 copy-done.4
  50.2 0.0 copy-done.5
  50.2 0.0 copy-done.6
  50.2 0.0 copy-start.10
  50.2 0.0 copy-start.11
  50.2 0.0 copy-start.12
  50.3 3.0 %convolve.1 = (bf16[1024,128]{1,0:T(8,128)(2,1)S(1)}, f32[8,128]{1,0:T(8,128)S(1)}) custom-call(bf16[2048,128]{1,0:T(8,128)(2,1)S(1)} %bitcast.12, f32[8,128]{1,0:T(8,128)S(1)} %bitcast.14, bf16[256,256]{1,0:T(8,128)(2,1)S(1)} %copy-done.5, bf16[256,256]{1,0:T(8,128)(2,1)S(1)} %copy-done.4, bf16[256,256]{1,0:T(8,128)(2,1)S(1)} %copy-done.3, ...), custom_call_target="tpu_custom_call" | custom-call | tf_op jit(solution)/shard_map/convolve/pallas_call | solution.py:147
  53.2 0.0 copy-start.7
  53.3 0.0 copy-start.8
  53.3 25.9 %all_to_all.16 = bf16[128,8,128]{2,1,0:T(8,128)(2,1)S(1)} all-to-all(bf16[128,8,128]{2,1,0:T(8,128)(2,1)S(1)} %bitcast.13), channel_id=1, replica_groups={{340,4,8,12,16,20,24,28,32,36,40,44,48,52,56,60,64,68,72,76,80,84,88,92..., dimensions={0} | all-to-all | bytes 524288 | tf_op jit(solution)/shard_map/all_to_all | solution.py:185
  79.1 0.0 copy-done.10
  79.1 0.0 copy-done.11
  79.1 0.0 copy-done.12
  79.1 0.0 copy-done.7
  79.1 0.0 copy-done.8
  79.2 0.3 multiply_reduce_fusion
  79.5 10.6 %all_to_all.17 = f32[4,1,128]{2,1,0:T(1,128)S(1)} all-to-all(f32[4,1,128]{2,1,0:T(1,128)S(1)} %broadcast_in_dim.2), channel_id=1, replica_groups={{2,1,0,3},{6,5,4,7},{10,9,8,11},{14,13,12,15},{18,17,16,19},{22,21,20,2..., dimensions={0} | all-to-all | bytes 4096 | tf_op jit(solution)/shard_map/all_to_all | solution.py:198
  90.1 1.0 %multiply_convert_fusion = (bf16[1024,128]{1,0:T(8,128)(2,1)}, bf16[1024,128]{1,0:T(8,128)(2,1)}) fusion(f32[1024,128]{1,0:T(8,128)S(1)} %get-tuple-element.7, f32[1024]{0:T(1024)S(1)} %bitcast.15, f32[128]{0:T(128)S(1)} %add_rsqrt_fusion), kind=kLoop, calls=%fused_computation.4 | loop fusion | flops 524288 | bytes 1053184 | tf_op jit(solution)/shard_map/convert_element_type | solution.py:209
  (3 shorter events, 0.0 us)
Async XLA Ops:
  0.6 1.2 %copy-start.9 = (bf16[1024,128]{1,0:T(8,128)(2,1)S(1)}, bf16[1024,128]{1,0:T(8,128)(2,1)}, u32[]{:S(2)}) copy-start(bf16[1024,128]{1,0:T(8,128)(2,1)} %param.16) | copy-start | bytes 786436
  1.9 48.3 %copy-start = (bf16[256,256]{1,0:T(8,128)(2,1)S(1)}, bf16[256,256]{1,0:T(8,128)(2,1)}, u32[]{:S(2)}) copy-start(bf16[256,256]{1,0:T(8,128)(2,1)} %constant.24.clone.leave_lo_ref) | copy-start | bytes 393220
  1.9 48.3 %copy-start.1 = (bf16[256,256]{1,0:T(8,128)(2,1)S(1)}, bf16[256,256]{1,0:T(8,128)(2,1)}, u32[]{:S(2)}) copy-start(bf16[256,256]{1,0:T(8,128)(2,1)} %constant.23.clone.leave_hi_ref) | copy-start | bytes 393220
  1.9 48.3 %copy-start.2 = (bf16[256,256]{1,0:T(8,128)(2,1)S(1)}, bf16[256,256]{1,0:T(8,128)(2,1)}, u32[]{:S(2)}) copy-start(bf16[256,256]{1,0:T(8,128)(2,1)} %constant.22.clone.back_ref) | copy-start | bytes 393220
  1.9 48.3 %copy-start.3 = (bf16[256,256]{1,0:T(8,128)(2,1)S(1)}, bf16[256,256]{1,0:T(8,128)(2,1)}, u32[]{:S(2)}) copy-start(bf16[256,256]{1,0:T(8,128)(2,1)} %constant.21.clone.over_lo_ref) | copy-start | bytes 393220
  1.9 48.2 %copy-start.4 = (bf16[256,256]{1,0:T(8,128)(2,1)S(1)}, bf16[256,256]{1,0:T(8,128)(2,1)}, u32[]{:S(2)}) copy-start(bf16[256,256]{1,0:T(8,128)(2,1)} %constant.20.clone.over_hi_ref) | copy-start | bytes 393220
  2.0 48.2 %copy-start.5 = (bf16[256,256]{1,0:T(8,128)(2,1)S(1)}, bf16[256,256]{1,0:T(8,128)(2,1)}, u32[]{:S(2)}) copy-start(bf16[256,256]{1,0:T(8,128)(2,1)} %constant.19.clone.enter_ref) | copy-start | bytes 393220
  2.0 48.2 %copy-start.6 = (f32[1024]{0:T(1024)S(1)}, f32[1024]{0:T(1024)}, u32[]{:S(2)}) copy-start(f32[1024]{0:T(1024)} %param.19) | copy-start | bytes 12292
  50.2 28.9 %copy-start.10 = (bf16[1024,128]{1,0:T(8,128)(2,1)S(1)}, bf16[1024,128]{1,0:T(8,128)(2,1)}, u32[]{:S(2)}) copy-start(bf16[1024,128]{1,0:T(8,128)(2,1)} %param.13) | copy-start | bytes 786436
  50.2 28.9 %copy-start.11 = (bf16[1024,128]{1,0:T(8,128)(2,1)S(1)}, bf16[1024,128]{1,0:T(8,128)(2,1)}, u32[]{:S(2)}) copy-start(bf16[1024,128]{1,0:T(8,128)(2,1)} %param.18) | copy-start | bytes 786436
  50.2 28.9 %copy-start.12 = (f32[1024]{0:T(1024)S(1)}, f32[1024]{0:T(1024)}, u32[]{:S(2)}) copy-start(f32[1024]{0:T(1024)} %param.17) | copy-start | bytes 12292
  53.2 25.9 %copy-start.7 = (bf16[1024,128]{1,0:T(8,128)(2,1)S(1)}, bf16[1024,128]{1,0:T(8,128)(2,1)}, u32[]{:S(2)}) copy-start(bf16[1024,128]{1,0:T(8,128)(2,1)} %param.15) | copy-start | bytes 786436
  53.3 25.9 %copy-start.8 = (bf16[1024,128]{1,0:T(8,128)(2,1)S(1)}, bf16[1024,128]{1,0:T(8,128)(2,1)}, u32[]{:S(2)}) copy-start(bf16[1024,128]{1,0:T(8,128)(2,1)} %param.14) | copy-start | bytes 786436

commit v7 on v6

--- a/solution.py
+++ b/solution.py
@@ -12,7 +12,7 @@
 BLOCKS = 128
 WIDTH = 128
 GROUP = 8
-LEAD = 85
+LEAD = 93
 CH_LEAD = 2
 SPAN = 256
 

time: 91.3 us -> 93 us (1.019)
  blocking collectives: 84.6 us -> 86.1 us
    all_to_all x1, blocking collectives: 25.9 us -> 27.1 us  [on_device(): lax.all_to_all(convolved.reshape(blocks, GROUP, width), 'seq', 0, 0, axis...]
where the time goes in v7:
time: 93 us; the launch traced here: 92.5 us
  blocking collectives  86.1 us (93%)
  Pallas kernels  2.97 us (3%)
  other arithmetic  2.56 us (3%)
    all_to_all x1, blocking collectives, on_device(): lax.all_to_all(both, 'seq', 0, 0, axis_index_groups=members, tiled=True)  48.8 us
    all_to_all x1, blocking collectives, on_device(): lax.all_to_all(convolved.reshape(blocks, GROUP, width), 'seq', 0, 0, axis...  27.1 us
    all_to_all x1, blocking collectives, on_device(): lax.all_to_all(jnp.broadcast_to(squares[None], (count, 1, width)), 'ch',...  10.2 us
    pallas_call x1, Pallas kernels, convolve(): pl.pallas_call(convolve_kernel, out_shape=(pltpu.VMEM((GROUP * BLOCKS, WI...  2.97 us

profile of v7, /device:TPU:1, one launch (start us, length us, event | category | flops | bytes accessed | tf_op | source)
XLA Modules:
  0.0 92.5 jit_solution(16227236486611815278)
XLA Ops:
  0.6 0.0 copy-start.9
  0.6 1.1 %fusion.3 = bf16[128,8,128]{2,1,0:T(8,128)(2,1)S(1)} fusion(bf16[1024,128]{1,0:T(8,128)(2,1)} %param.15, bf16[1024,128]{1,0:T(8,128)(2,1)} %param.14), kind=kLoop, calls=%fused_computation.8 | loop fusion | flops 655360 | bytes 786432 | tf_op jit(solution)/shard_map/reshape | solution.py:175
  1.8 0.0 copy-done.9
  1.8 0.1 pad_maximum_fusion
  1.9 0.0 copy-start
  1.9 0.0 copy-start.1
  1.9 0.0 copy-start.2
  1.9 0.0 copy-start.3
  1.9 0.0 copy-start.4
  2.0 0.0 copy-start.5
  2.0 0.0 copy-start.6
  2.0 48.8 %all_to_all.15 = bf16[128,16,128]{2,1,0:T(8,128)(2,1)S(1)} all-to-all(bf16[128,16,128]{2,1,0:T(8,128)(2,1)S(1)} %pad_maximum_fusion), channel_id=1, replica_groups={{372,4,8,12,16,20,24,28,32,36,40,44,48,52,56,60,64,68,72,76,80,84,88,92..., dimensions={0} | all-to-all | bytes 1048576 | tf_op jit(solution)/shard_map/all_to_all | solution.py:179
  50.8 0.0 copy-done
  50.8 0.0 copy-done.1
  50.8 0.0 copy-done.2
  50.8 0.0 copy-done.3
  50.9 0.0 copy-done.4
  50.9 0.0 copy-done.5
  50.9 0.0 copy-done.6
  50.9 0.0 copy-start.10
  50.9 0.0 copy-start.11
  50.9 0.0 copy-start.12
  50.9 3.0 %convolve.1 = (bf16[1024,128]{1,0:T(8,128)(2,1)S(1)}, f32[8,128]{1,0:T(8,128)S(1)}) custom-call(bf16[2048,128]{1,0:T(8,128)(2,1)S(1)} %bitcast.12, f32[8,128]{1,0:T(8,128)S(1)} %bitcast.14, bf16[256,256]{1,0:T(8,128)(2,1)S(1)} %copy-done.5, bf16[256,256]{1,0:T(8,128)(2,1)S(1)} %copy-done.4, bf16[256,256]{1,0:T(8,128)(2,1)S(1)} %copy-done.3, ...), custom_call_target="tpu_custom_call" | custom-call | tf_op jit(solution)/shard_map/convolve/pallas_call | solution.py:147
  53.9 0.0 copy-start.7
  53.9 0.0 copy-start.8
  53.9 27.1 %all_to_all.16 = bf16[128,8,128]{2,1,0:T(8,128)(2,1)S(1)} all-to-all(bf16[128,8,128]{2,1,0:T(8,128)(2,1)S(1)} %bitcast.13), channel_id=1, replica_groups={{372,4,8,12,16,20,24,28,32,36,40,44,48,52,56,60,64,68,72,76,80,84,88,92..., dimensions={0} | all-to-all | bytes 524288 | tf_op jit(solution)/shard_map/all_to_all | solution.py:185
  81.0 0.0 copy-done.10
  81.0 0.0 copy-done.11
  81.0 0.0 copy-done.12
  81.0 0.0 copy-done.7
  81.0 0.0 copy-done.8
  81.0 0.3 multiply_reduce_fusion
  81.4 10.2 %all_to_all.17 = f32[4,1,128]{2,1,0:T(1,128)S(1)} all-to-all(f32[4,1,128]{2,1,0:T(1,128)S(1)} %broadcast_in_dim.2), channel_id=1, replica_groups={{2,1,0,3},{6,5,4,7},{10,9,8,11},{14,13,12,15},{18,17,16,19},{22,21,20,2..., dimensions={0} | all-to-all | bytes 4096 | tf_op jit(solution)/shard_map/all_to_all | solution.py:198
  91.6 1.0 %multiply_convert_fusion = (bf16[1024,128]{1,0:T(8,128)(2,1)}, bf16[1024,128]{1,0:T(8,128)(2,1)}) fusion(f32[1024,128]{1,0:T(8,128)S(1)} %get-tuple-element.7, f32[1024]{0:T(1024)S(1)} %bitcast.15, f32[128]{0:T(128)S(1)} %add_rsqrt_fusion), kind=kLoop, calls=%fused_computation.4 | loop fusion | flops 524288 | bytes 1053184 | tf_op jit(solution)/shard_map/convert_element_type | solution.py:209
  (3 shorter events, 0.0 us)
Async XLA Ops:
  0.6 1.2 %copy-start.9 = (bf16[1024,128]{1,0:T(8,128)(2,1)S(1)}, bf16[1024,128]{1,0:T(8,128)(2,1)}, u32[]{:S(2)}) copy-start(bf16[1024,128]{1,0:T(8,128)(2,1)} %param.16) | copy-start | bytes 786436
  1.9 48.9 %copy-start = (bf16[256,256]{1,0:T(8,128)(2,1)S(1)}, bf16[256,256]{1,0:T(8,128)(2,1)}, u32[]{:S(2)}) copy-start(bf16[256,256]{1,0:T(8,128)(2,1)} %constant.24.clone.leave_lo_ref) | copy-start | bytes 393220
  1.9 48.9 %copy-start.1 = (bf16[256,256]{1,0:T(8,128)(2,1)S(1)}, bf16[256,256]{1,0:T(8,128)(2,1)}, u32[]{:S(2)}) copy-start(bf16[256,256]{1,0:T(8,128)(2,1)} %constant.23.clone.leave_hi_ref) | copy-start | bytes 393220
  1.9 48.9 %copy-start.2 = (bf16[256,256]{1,0:T(8,128)(2,1)S(1)}, bf16[256,256]{1,0:T(8,128)(2,1)}, u32[]{:S(2)}) copy-start(bf16[256,256]{1,0:T(8,128)(2,1)} %constant.22.clone.back_ref) | copy-start | bytes 393220
  1.9 48.9 %copy-start.3 = (bf16[256,256]{1,0:T(8,128)(2,1)S(1)}, bf16[256,256]{1,0:T(8,128)(2,1)}, u32[]{:S(2)}) copy-start(bf16[256,256]{1,0:T(8,128)(2,1)} %constant.21.clone.over_lo_ref) | copy-start | bytes 393220
  1.9 48.9 %copy-start.4 = (bf16[256,256]{1,0:T(8,128)(2,1)S(1)}, bf16[256,256]{1,0:T(8,128)(2,1)}, u32[]{:S(2)}) copy-start(bf16[256,256]{1,0:T(8,128)(2,1)} %constant.20.clone.over_hi_ref) | copy-start | bytes 393220
  2.0 48.9 %copy-start.5 = (bf16[256,256]{1,0:T(8,128)(2,1)S(1)}, bf16[256,256]{1,0:T(8,128)(2,1)}, u32[]{:S(2)}) copy-start(bf16[256,256]{1,0:T(8,128)(2,1)} %constant.19.clone.enter_ref) | copy-start | bytes 393220
  2.0 48.9 %copy-start.6 = (f32[1024]{0:T(1024)S(1)}, f32[1024]{0:T(1024)}, u32[]{:S(2)}) copy-start(f32[1024]{0:T(1024)} %param.19) | copy-start | bytes 12292
  50.9 30.1 %copy-start.10 = (bf16[1024,128]{1,0:T(8,128)(2,1)S(1)}, bf16[1024,128]{1,0:T(8,128)(2,1)}, u32[]{:S(2)}) copy-start(bf16[1024,128]{1,0:T(8,128)(2,1)} %param.13) | copy-start | bytes 786436
  50.9 30.1 %copy-start.11 = (bf16[1024,128]{1,0:T(8,128)(2,1)S(1)}, bf16[1024,128]{1,0:T(8,128)(2,1)}, u32[]{:S(2)}) copy-start(bf16[1024,128]{1,0:T(8,128)(2,1)} %param.18) | copy-start | bytes 786436
  50.9 30.1 %copy-start.12 = (f32[1024]{0:T(1024)S(1)}, f32[1024]{0:T(1024)}, u32[]{:S(2)}) copy-start(f32[1024]{0:T(1024)} %param.17) | copy-start | bytes 12292
  53.9 27.1 %copy-start.7 = (bf16[1024,128]{1,0:T(8,128)(2,1)S(1)}, bf16[1024,128]{1,0:T(8,128)(2,1)}, u32[]{:S(2)}) copy-start(bf16[1024,128]{1,0:T(8,128)(2,1)} %param.15) | copy-start | bytes 786436
  53.9 27.1 %copy-start.8 = (bf16[1024,128]{1,0:T(8,128)(2,1)S(1)}, bf16[1024,128]{1,0:T(8,128)(2,1)}, u32[]{:S(2)}) copy-start(bf16[1024,128]{1,0:T(8,128)(2,1)} %param.14) | copy-start | bytes 786436
